TPU v7x, 16 devices: a whole 2x2x2 slice. The times are simulated.
16 devices in a mesh: dp: 16 (over z, y, x, core).
Axes of the slice: x: 2, y: 2, z: 2, core: 2. Of those that a mesh axis runs over, the one named last changes fastest.
Arguments:
- query_feat: bfloat16 [8192, 512], P('dp')
- item_feat: bfloat16 [8192, 512], P('dp')
- log_q: float32 [8192], P('dp')
- w_query_in: bfloat16 [512, 256], replicated
- w_query_out: bfloat16 [256, 128], replicated
- w_item_in: bfloat16 [512, 256], replicated
- w_item_out: bfloat16 [256, 128], replicated
Outputs:
- output 1: float32 [1], replicated
- output 2: float32 [512, 256], replicated
- output 3: float32 [256, 128], replicated
- output 4: float32 [512, 256], replicated
- output 5: float32 [256, 128], replicated
All inputs are finite; a program needn't handle non-finite values.
Results may differ from a plain program's by a relative error of at most 0.0074964.
Values are sent between devices in bfloat16 or wider.
A program may use at most 1 GiB of HBM per device.

v0:
```python
import jax
import jax.numpy as jnp
from jax import lax
from jax.sharding import PartitionSpec as P

value_a11 = 0.05
NORM_EPS = 1e-6


def tower_forward(feat_rows, w_in, w_out):
    pre_act = jnp.dot(feat_rows, w_in, preferred_element_type=jnp.float32)
    hidden = jnp.maximum(pre_act, 0.0).astype(jnp.bfloat16)
    embed = jnp.dot(hidden, w_out, preferred_element_type=jnp.float32)
    inv_norm = lax.rsqrt(jnp.sum(embed * embed, axis=-1, keepdims=True) + NORM_EPS)
    return pre_act, hidden, inv_norm, embed * inv_norm


def tower_backward(feat_rows, w_out, pre_act, hidden, inv_norm, unit_vec, d_unit):
    d_embed = inv_norm * (d_unit - unit_vec * jnp.sum(unit_vec * d_unit, axis=-1, keepdims=True))
    d_embed_bf = d_embed.astype(jnp.bfloat16)
    grad_out = jnp.einsum('bh,be->he', hidden, d_embed_bf, preferred_element_type=jnp.float32)
    d_hidden = jnp.einsum('be,he->bh', d_embed_bf, w_out, preferred_element_type=jnp.float32)
    d_pre = jnp.where(pre_act > 0, d_hidden, 0.0).astype(jnp.bfloat16)
    grad_in = jnp.einsum('bf,bh->fh', feat_rows, d_pre, preferred_element_type=jnp.float32)
    return grad_in, grad_out


def softmax_grads(query_bf, items_all, logq_all, row_offset):
    local_rows, embed_dim = query_bf.shape
    total_rows = items_all.shape[0]
    block_rows = min(local_rows, 256)
    num_blocks = local_rows // block_rows
    grad_scale = 1.0 / (value_a11 * total_rows)
    col_ids = lax.broadcasted_iota(jnp.int32, (1, total_rows), 1)
    row_iota = lax.broadcasted_iota(jnp.int32, (block_rows, 1), 0)
    query_blocks = query_bf.reshape(num_blocks, block_rows, embed_dim)

    def block_step(d_item_acc, inputs):
        block_index, query_blk = inputs
        logits = jnp.einsum('qe,ke->qk', query_blk, items_all, preferred_element_type=jnp.float32) / value_a11 - logq_all[None, :]
        is_pos = (row_offset + block_index * block_rows + row_iota) == col_ids
        row_max = jnp.max(logits, axis=1, keepdims=True)
        log_norm = row_max + jnp.log(jnp.sum(jnp.exp(logits - row_max), axis=1, keepdims=True))
        pos_logit = jnp.sum(jnp.where(is_pos, logits, 0.0), axis=1, keepdims=True)
        prob_rows = jnp.exp(logits - log_norm)
        grad_logits = jnp.where(is_pos, prob_rows - 1.0, prob_rows).astype(jnp.bfloat16)
        d_query_blk = jnp.einsum('qk,ke->qe', grad_logits, items_all, preferred_element_type=jnp.float32) * grad_scale
        d_item_acc = d_item_acc + jnp.einsum('qk,qe->ke', grad_logits, query_blk, preferred_element_type=jnp.float32)
        return d_item_acc, (jnp.sum(log_norm - pos_logit), d_query_blk)

    acc_init = jnp.zeros((total_rows, embed_dim), jnp.float32)
    d_item_acc, (loss_parts, d_query_blocks) = lax.scan(block_step, acc_init, (jnp.arange(num_blocks), query_blocks))
    return jnp.sum(loss_parts), d_query_blocks.reshape(local_rows, embed_dim), d_item_acc * grad_scale


def solution(mesh):
    group = mesh.shape['dp']

    def local_step(query_feat, item_feat, log_q, w_query_in, w_query_out, w_item_in, w_item_out):
        local_rows = query_feat.shape[0]
        total_rows = local_rows * group
        q_pre, q_hidden, q_inv, q_unit = tower_forward(query_feat, w_query_in, w_query_out)
        v_pre, v_hidden, v_inv, v_unit = tower_forward(item_feat, w_item_in, w_item_out)
        items_all = lax.all_gather(v_unit.astype(jnp.bfloat16), 'dp', axis=0, tiled=True)
        logq_all = lax.all_gather(log_q, 'dp', axis=0, tiled=True)
        row_offset = lax.axis_index('dp') * local_rows
        loss_sum, d_query, d_item_part = softmax_grads(q_unit.astype(jnp.bfloat16), items_all, logq_all, row_offset)
        d_item = lax.psum_scatter(d_item_part, 'dp', scatter_dimension=0, tiled=True)
        grad_query_in, grad_query_out = tower_backward(query_feat, w_query_out, q_pre, q_hidden, q_inv, q_unit, d_query)
        grad_item_in, grad_item_out = tower_backward(item_feat, w_item_out, v_pre, v_hidden, v_inv, v_unit, d_item)
        loss = jnp.reshape(lax.psum(loss_sum, 'dp') / total_rows, (1,))
        return (loss, lax.psum(grad_query_in, 'dp'), lax.psum(grad_query_out, 'dp'), lax.psum(grad_item_in, 'dp'), lax.psum(grad_item_out, 'dp'))

    return jax.shard_map(local_step, mesh=mesh, in_specs=(P('dp', None), P('dp', None), P('dp'), P(), P(), P(), P()), out_specs=(P(), P(), P(), P(), P()), check_vma=False)
```

profile of v0, /device:TPU:0, one launch (start us, length us, event | category | flops | bytes accessed | tf_op | source)
XLA Modules:
  0.0 261.1 jit_solution(15887054215170247782)
XLA Ops:
  7.2 1.4 fusion.37
  8.7 1.1 multiply_reduce_fusion.1
  10.6 15.1 %all-gather = f32[16,1,512]{2,1,0:T(1,128)} all-gather(f32[1,1,512]{2,1,0:T(1,128)} %bitcast.73), channel_id=1, replica_groups=mesh['dp'=16] {'dp'}, dimensions={0}, use_global_device_ids=true | all-gather | bytes 34816 | tf_op jit(solution)/shard_map/all_gather | solution.py:65
  25.7 1.2 fusion.36
  27.8 1.2 multiply_reduce_fusion.2
  29.8 13.0 %all-gather.3.cloned.1.call-done = bf16[8192,128]{0,1:T(8,128)(2,1)} async-done(((bf16[512,128]{0,1:T(8,128)(2,1)}), bf16[8192,128]{0,1:T(8,128)(2,1)}) %all-gather.3.cloned.1.call-update) | async-done | bytes 2097168 | tf_op jit(solution)/shard_map/all_gather | solution.py:64
  42.8 3.2 %copy.20 = bf16[8192,128]{1,0:T(8,128)(2,1)S(1)} copy(bf16[8192,128]{0,1:T(8,128)(2,1)} %all-gather.3.cloned.1.call-done) | data formatting | bytes 4194304
  46.0 51.8 %while.17 = (s32[]{:T(128)}, f32[8192,128]{1,0:T(8,128)}, f32[2]{0:T(128)}, f32[2,256,128]{2,1,0:T(8,128)}, s32[2]{0:T(128)S(1)}, /*index=5*/s32[]{:T(128)}, bf1...) while((s32[]{:T(128)}, f32[8192,128]{1,0:T(8,128)}, ...), condition=%wide.region_7.8_spmd.clone, body=%wide.region_2.7_spmd.clone.sunk | while | flops 1640005888 | bytes 103068080 | solution.py:52
  46.1 5.2 %fusion.70 = (f32[256]{0:T(256)S(1)}, f32[256,8192]{1,0:T(8,128)}) fusion(f32[8192]{0:T(1024)} %get-tuple-element.354, bf16[8192,128]{1,0:T(8,128)(2,1)S(1)} %get-tuple-element.353, bf16[2,256,128]{2,1,0:T(8,128)(2,1)S(1)} %get-tuple-element.352, s32[]{:T(128)} %get-tuple-element.334), kind=kOutput, calls=%fused_computation.59.clone.1 | convolution fusion | flops 543162112 | bytes 10585092 | tf_op jit(solution)/shard_map/while/body/eval_jaxpr/qe,ke->qk/dot_general | solution.py:40
  52.6 5.8 %fusion.71 = (f32[256]{0:T(256)S(1)}, f32[256]{0:T(256)S(1)}) fusion(f32[256,8192]{1,0:T(8,128)} %get-tuple-element.316, s32[256]{0:T(256)S(1)} %bitcast.71, f32[256]{0:T(256)S(1)} %get-tuple-element.317), kind=kLoop, calls=%fused_computation.9.clone.1 | loop fusion | flops 10485248 | bytes 8392704 | tf_op jit(solution)/shard_map/while/body/eval_jaxpr/reduce_sum | solution.py:44
  59.0 3.4 %fusion.72 = bf16[256,8192]{1,0:T(8,128)(2,1)} fusion(f32[256,8192]{1,0:T(8,128)S(1)} %copy-done.1, f32[256]{0:T(256)S(1)} %get-tuple-element.320, s32[256]{0:T(256)S(1)} %bitcast.72), kind=kLoop, calls=%fused_computation.6.clone.1 | loop fusion | flops 10485760 | bytes 12584960 | tf_op jit(solution)/shard_map/while/body/eval_jaxpr/convert_element_type | solution.py:46
  62.3 5.7 %convolution_add_fusion.2 = f32[8192,128]{1,0:T(8,128)} fusion(bf16[256,8192]{1,0:T(8,128)(2,1)} %fusion.72, f32[8192,128]{1,0:T(8,128)} %get-tuple-element.335, pred[]{:T(512)S(6)} %compare.3, bf16[2,256,128]{2,1,0:T(8,128)(2,1)S(1)} %get-tuple-element.352, s32[]{:T(128)} %get-tuple-element.334), kind=kOutput, calls=%fused_computation.5.clone.1 | convolution fusion | flops 538968064 | bytes 12648453 | tf_op jit(solution)/shard_map/while/body/eval_jaxpr/qk,qe->ke/dot_general | solution.py:48
  68.0 1.3 fusion.73
  71.4 5.2 %fusion.70 = (f32[256]{0:T(256)S(1)}, f32[256,8192]{1,0:T(8,128)}) fusion(f32[8192]{0:T(1024)} %get-tuple-element.354, bf16[8192,128]{1,0:T(8,128)(2,1)S(1)} %get-tuple-element.353, bf16[2,256,128]{2,1,0:T(8,128)(2,1)S(1)} %get-tuple-element.352, s32[]{:T(128)} %get-tuple-element.334), kind=kOutput, calls=%fused_computation.59.clone.1 | convolution fusion | flops 543162112 | bytes 10585092 | tf_op jit(solution)/shard_map/while/body/eval_jaxpr/qe,ke->qk/dot_general | solution.py:40
  77.9 5.8 %fusion.71 = (f32[256]{0:T(256)S(1)}, f32[256]{0:T(256)S(1)}) fusion(f32[256,8192]{1,0:T(8,128)} %get-tuple-element.316, s32[256]{0:T(256)S(1)} %bitcast.71, f32[256]{0:T(256)S(1)} %get-tuple-element.317), kind=kLoop, calls=%fused_computation.9.clone.1 | loop fusion | flops 10485248 | bytes 8392704 | tf_op jit(solution)/shard_map/while/body/eval_jaxpr/reduce_sum | solution.py:44
  84.3 3.4 %fusion.72 = bf16[256,8192]{1,0:T(8,128)(2,1)} fusion(f32[256,8192]{1,0:T(8,128)S(1)} %copy-done.1, f32[256]{0:T(256)S(1)} %get-tuple-element.320, s32[256]{0:T(256)S(1)} %bitcast.72), kind=kLoop, calls=%fused_computation.6.clone.1 | loop fusion | flops 10485760 | bytes 12584960 | tf_op jit(solution)/shard_map/while/body/eval_jaxpr/convert_element_type | solution.py:46
  87.6 6.9 %convolution_add_fusion.2 = f32[8192,128]{1,0:T(8,128)} fusion(bf16[256,8192]{1,0:T(8,128)(2,1)} %fusion.72, f32[8192,128]{1,0:T(8,128)} %get-tuple-element.335, pred[]{:T(512)S(6)} %compare.3, bf16[2,256,128]{2,1,0:T(8,128)(2,1)S(1)} %get-tuple-element.352, s32[]{:T(128)} %get-tuple-element.334), kind=kOutput, calls=%fused_computation.5.clone.1 | convolution fusion | flops 538968064 | bytes 12648453 | tf_op jit(solution)/shard_map/while/body/eval_jaxpr/qk,qe->ke/dot_general | solution.py:48
  94.5 1.3 fusion.73
  97.9 5.6 %copy.21 = f32[8192,128]{0,1:T(8,128)} copy(f32[8192,128]{1,0:T(8,128)} %get-tuple-element.146) | data formatting | bytes 8388608 | tf_op jit(solution)/shard_map/while | solution.py:52
  103.5 4.5 %broadcast_multiply_fusion = f32[8192,128]{0,1:T(8,128)} fusion(f32[8192,128]{0,1:T(8,128)} %copy.21), kind=kLoop, calls=%fused_computation.23 | loop fusion | flops 1048576 | bytes 8388608 | tf_op jit(solution)/shard_map/mul | solution.py:53
  110.4 1.4 convolution_bitcast_fusion.1
  111.8 60.2 %reduce-scatter.2.cloned.1.call-done = f32[512,128]{0,1:T(8,128)} async-done(((f32[8192,128]{0,1:T(8,128)}), f32[512,128]{0,1:T(8,128)}) %reduce-scatter.2.cloned.1.call-update) | async-done | bytes 262160 | tf_op jit(solution)/shard_map/reduce_scatter | solution.py:68
  172.0 1.0 multiply_reduce_fusion
  173.0 1.0 multiply_convert_fusion
  174.0 0.9 fusion.27
  175.0 1.4 convolution_bitcast_fusion
  177.0 31.2 %psum.35 = f32[]{:T(128)} all-reduce(f32[]{:T(128)} %reduce_sum.83), channel_id=1, replica_groups=mesh['dp'=16] {'dp'}, use_global_device_ids=true, to_apply=%region_9.10 | all-reduce | flops 1 | bytes 8 | tf_op jit(solution)/shard_map/psum | solution.py:71
  208.9 37.3 %all-reduce.3.cloned.1.call-done = (f32[512,256]{0,1:T(8,128)}, f32[256,128]{1,0:T(8,128)}, f32[512,256]{0,1:T(8,128)}, f32[256,128]{1,0:T(8,128)}) async-done(((f32[512,256]{0,1:T(8,128)}, f32[256,128]{1,0:T(8,128)}, f32[512,256]{0,1:T(8,128)}, f32[256,128]{1,0:T(8,128)}), (f32[512,256]{0,1:T(8,128)}, f32[256,128]{1,0:T(8,128)}, f32[512,256]{0,1:T(8,128)}, ...) | async-done | bytes 1310736 | tf_op jit(solution)/shard_map/psum | solution.py:72
  246.2 2.0 copy.22
  248.3 2.0 copy.23
  250.3 1.6 copy.42
  251.9 1.6 copy.43
  (70 shorter events, 11.9 us)
Async XLA Ops:
  7.2 18.6 %copy-start = (bf16[512,512]{1,0:T(8,128)(2,1)S(1)}, bf16[512,512]{1,0:T(8,128)(2,1)}, u32[]{:S(2)}) copy-start(bf16[512,512]{1,0:T(8,128)(2,1)} %param.9) | copy-start | bytes 1572868
  7.2 35.6 %all-gather.3.cloned.1.call-start = ((), (), s32[]{:S(2)}) async-start(), calls=%async_computation.1 | async-start | bytes 2228224 | tf_op jit(solution)/shard_map/all_gather | solution.py:64
  10.5 161.5 %reduce-scatter.2.cloned.1.call-start = ((), (), s32[]{:S(2)}) async-start(), calls=%async_computation.2 | async-start | bytes 4456448 | tf_op jit(solution)/shard_map/reduce_scatter | solution.py:68
  27.0 0.8 copy-start.3
  28.9 0.7 copy-start.5
  52.6 6.4 %copy-start.1 = (f32[256,8192]{1,0:T(8,128)S(1)}, f32[256,8192]{1,0:T(8,128)}, u32[]{:S(2)}) copy-start(f32[256,8192]{1,0:T(8,128)} %get-tuple-element.316) | copy-start | bytes 25165828 | tf_op jit(solution)/shard_map/while
  62.3 5.7 %copy-start.2 = (bf16[256,8192]{1,0:T(8,128)(2,1)S(1)}, bf16[256,8192]{1,0:T(8,128)(2,1)}, u32[]{:S(2)}) copy-start(bf16[256,8192]{1,0:T(8,128)(2,1)} %fusion.72) | copy-start | bytes 12582916 | tf_op jit(solution)/shard_map/while
  62.3 5.7 %copy-start.8 = (f32[2,256,128]{2,1,0:T(8,128)S(1)}, f32[2,256,128]{2,1,0:T(8,128)}, u32[]{:S(2)}) copy-start(f32[2,256,128]{2,1,0:T(8,128)} %get-tuple-element.337) | copy-start | bytes 786436 | tf_op jit(solution)/shard_map/while
  68.0 2.0 copy-start.13
  69.3 0.7 copy-start.9
  70.8 0.6 copy-start.14
  77.8 6.4 %copy-start.1 = (f32[256,8192]{1,0:T(8,128)S(1)}, f32[256,8192]{1,0:T(8,128)}, u32[]{:S(2)}) copy-start(f32[256,8192]{1,0:T(8,128)} %get-tuple-element.316) | copy-start | bytes 25165828 | tf_op jit(solution)/shard_map/while
  87.6 6.9 %copy-start.2 = (bf16[256,8192]{1,0:T(8,128)(2,1)S(1)}, bf16[256,8192]{1,0:T(8,128)(2,1)}, u32[]{:S(2)}) copy-start(bf16[256,8192]{1,0:T(8,128)(2,1)} %fusion.72) | copy-start | bytes 12582916 | tf_op jit(solution)/shard_map/while
  87.6 6.9 %copy-start.8 = (f32[2,256,128]{2,1,0:T(8,128)S(1)}, f32[2,256,128]{2,1,0:T(8,128)}, u32[]{:S(2)}) copy-start(f32[2,256,128]{2,1,0:T(8,128)} %get-tuple-element.337) | copy-start | bytes 786436 | tf_op jit(solution)/shard_map/while
  94.5 2.0 copy-start.13
  95.8 0.7 copy-start.9
  97.3 0.6 copy-start.14
  108.0 0.9 copy-start.6
  108.0 1.0 copy-start.10
  108.0 1.5 copy-start.4
  108.0 2.4 copy-start.11
  108.0 66.9 %copy-start.7 = (bf16[512,512]{1,0:T(8,128)(2,1)S(1)}, bf16[512,512]{1,0:T(8,128)(2,1)}, u32[]{:S(2)}) copy-start(bf16[512,512]{1,0:T(8,128)(2,1)} %param.10) | copy-start | bytes 1572868
  108.0 66.9 %copy-start.12 = (bf16[256,128]{1,0:T(8,128)(2,1)S(1)}, bf16[256,128]{1,0:T(8,128)(2,1)}, u32[]{:S(2)}) copy-start(bf16[256,128]{1,0:T(8,128)(2,1)} %param.15) | copy-start | bytes 196612
  108.1 138.1 %all-reduce.3.cloned.1.call-start = ((), (), s32[]{:S(2)}) async-start(), calls=%async_computation.3 | async-start | bytes 2621440 | tf_op jit(solution)/shard_map/psum | solution.py:72
  109.3 67.1 %copy-start.15 = (f32[2]{0:T(128)S(1)}, f32[2]{0:T(128)}, u32[]{:S(2)}) copy-start(f32[2]{0:T(128)} %get-tuple-element.144) | copy-start | bytes 28
Sparse Core Ops, SparseCore 0:
  10.8 31.9 all-gather.2
  108.2 63.7 reduce-scatter.1
  177.6 68.5 all-reduce.2
where the time goes:
time: 262 us; the launch traced here: 261 us
  waiting for transfers between devices  111 us (42%)
  blocking collectives  46.4 us (18%)
  matrix products  35.2 us (13%)
  other arithmetic  27.9 us (11%)
  local copies, waits for them, and re-layouts  23.8 us (9%)
  between operations  15.7 us (6%)
    reduce_scatter x1, waiting for transfers between devices, local_step(): lax.psum_scatter(d_item_part, 'dp', scatter_dimension=0, tiled=True)  60.2 us
    psum x1, waiting for transfers between devices, local_step(): lax.psum(grad_query_in, 'dp')  37.3 us
    psum x1, blocking collectives, local_step(): loss = jnp.reshape(lax.psum(loss_sum, 'dp') / total_rows, (1,))  31.2 us
    all_gather x1, blocking collectives, local_step(): logq_all = lax.all_gather(log_q, 'dp', axis=0, tiled=True)  15.1 us
    all_gather x1, waiting for transfers between devices, local_step(): lax.all_gather(v_unit.astype(jnp.bfloat16), 'dp', axis=0, tiled=True)  13 us
    unnamed x25, local copies, waits for them, and re-layouts  12.9 us
    dot_general x2, matrix products, block_step(): jnp.einsum('qk,qe->ke', grad_logits, query_blk, preferred_element_type=jn...  12.6 us
    reduce_sum x2, other arithmetic, block_step(): pos_logit = jnp.sum(jnp.where(is_pos, logits, 0.0), axis=1, keepdims=True)  11.6 us
  transfers between devices with their start and end apart: 3, of which 3 were waited for; matrix products, arithmetic and copies ran while one was open for 2% of the time, Pallas kernels for 0%

commit v1 on v0

v1 whole, which is shorter than its diff:
```python
import jax
import jax.numpy as jnp
from jax import lax
from jax.experimental import pallas as pl
from jax.experimental.pallas import tpu as pltpu
from jax.sharding import PartitionSpec as P

MESH = pl.DeviceIdType.MESH
TEMPERATURE = 0.05
NORM_EPS = 1e-6
LOG2E = 1.4426950408889634
NDEV = 16
ROWS = 512
FEAT = 512
HID = 256
EMB = 128
TOTAL = NDEV * ROWS
GRAD_SCALE = 1.0 / (TEMPERATURE * TOTAL)
LOGIT_SCALE = LOG2E / TEMPERATURE
PARTS = ((0, 176), (176, 176), (352, 160))
ORDERS = ((1, 2, 4), (2, 4, 1), (4, 1, 2))
LEVELS = ((1, 2, 4), (6, 5, 3), (7,))
MSG = ROWS + 128
F32 = jnp.float32
BF16 = jnp.bfloat16


def dot_nn(a, b):
    return lax.dot_general(a, b, (((1,), (0,)), ((), ())), preferred_element_type=F32)


def dot_nt(a, b):
    return lax.dot_general(a, b, (((1,), (1,)), ((), ())), preferred_element_type=F32)


def dot_tn(a, b):
    return lax.dot_general(a, b, (((0,), (0,)), ((), ())), preferred_element_type=F32)


def kernel(qx, vx, lq, wqi, wqo, wvi, wvo,
           loss_out, gqi_out, gqo_out, gvi_out, gvo_out,
           uall, vall, lqall, brow, msgs, exps, lacc,
           a_q, a_v, h_q, h_v, u_q, u_v, r_q, r_v, invl, bcol, dacc,
           pi_q, po_q, pi_v, po_v, ri_q, ro_q, ri_v, ro_v,
           s_lq, m_lq, s_msg, m_msg,
           s_v, m_v, s_vd, m_vd, s_u, m_u, s_ud, m_ud,
           s_pair, m_pair, s_rs, m_rs, s_ag, m_ag, s_fw, m_fw):
    me = lax.axis_index("dp")
    core = me % 2
    bit_x, bit_y, bit_z = (me // 2) % 2, (me // 4) % 2, (me // 8) % 2
    step_x, step_y, step_z = 2 - 4 * bit_x, 4 - 8 * bit_y, 8 - 16 * bit_z
    partner = me + 1 - 2 * core
    chip = me // 2

    def dev(mask):
        return me + (mask % 2) * step_x + ((mask // 2) % 2) * step_y + (mask // 4) * step_z

    def dev_other(mask):
        return partner + (mask % 2) * step_x + ((mask // 2) % 2) * step_y + (mask // 4) * step_z

    def rcopy(src, dst, ssem, rsem, to):
        return pltpu.make_async_remote_copy(src_ref=src, dst_ref=dst, send_sem=ssem, recv_sem=rsem,
                                            device_id=(to,), device_id_type=MESH)

    pending = []

    def send(src, dst, ssem, rsem, to):
        copy = rcopy(src, dst, ssem, rsem, to)
        copy.start()
        pending.append(copy)

    def arrived(ref, rsem):
        rcopy(ref, ref, rsem, rsem, partner).wait_recv()

    others = [(me + k) % NDEV for k in range(1, NDEV)]

    barrier = pltpu.get_barrier_semaphore()
    for k in range(NDEV - 1):
        pl.semaphore_signal(barrier, inc=1, device_id=(others[k],), device_id_type=MESH)

    def tower_forward(x, w_in, w_out, a_ref, h_ref, u_ref, r_ref, all_ref):
        a = dot_nn(x[...], w_in[...])
        a_ref[...] = a
        h = jnp.maximum(a, 0.0).astype(BF16)
        h_ref[...] = h
        e = dot_nn(h, w_out[...])
        r = lax.rsqrt(jnp.sum(e * e, axis=-1, keepdims=True) + NORM_EPS)
        u = e * r
        u_ref[...] = u
        r_ref[...] = jnp.broadcast_to(r, (ROWS, EMB))
        all_ref[me] = u.astype(BF16)

    lqall[me] = lq[...]
    tower_forward(vx, wvi, wvo, a_v, h_v, u_v, r_v, vall)
    pl.semaphore_wait(barrier, NDEV - 1)

    for k in range(NDEV - 1):
        send(lq, lqall.at[me], s_lq.at[k], m_lq.at[k], others[k])

    def part_ref(ref, src, p):
        return ref.at[src, pl.ds(PARTS[p][0], PARTS[p][1]), :]

    def gather_own(ref, ss, ms, sd, md):
        send(ref.at[me], ref.at[me], sd.at[0], md.at[0], partner)
        for t in range(3):
            for p in range(3):
                d = ORDERS[p][t]
                send(part_ref(ref, me, p), part_ref(ref, me, p), ss.at[p, 0, t], ms.at[p, d], dev(d))

    def gather_level(ref, level, ss, ms, sd, md):
        jobs = []
        for p in range(3):
            for m in LEVELS[level]:
                top = max(t for t in range(3) if ORDERS[p][t] & m)
                jobs.append((top, p, m))
        for top, p, m in sorted(jobs):
            src = dev(m)
            arrived(part_ref(ref, src, p), ms.at[p, m])
            for t in range(top + 1, 3):
                d = ORDERS[p][t]
                send(part_ref(ref, src, p), part_ref(ref, src, p), ss.at[p, m, t], ms.at[p, m + d], dev(d))
        for m in LEVELS[level]:
            send(ref.at[dev(m)], ref.at[dev(m)], sd.at[m], md.at[m], partner)

    def gather_pair(ref, masks, md):
        for m in masks:
            arrived(ref.at[dev_other(m)], md.at[m])

    gather_own(vall, s_v, m_v, s_vd, m_vd)

    tower_forward(qx, wqi, wqo, a_q, h_q, u_q, r_q, uall)

    for k in range(NDEV - 1):
        src = (me + NDEV - 1 - k) % NDEV
        arrived(lqall.at[src], m_lq.at[k])
    shift = jnp.max(-lqall[...])
    brow[...] = (lqall[...] + shift) * LOG2E
    bcol[...] = jnp.broadcast_to((lq[...] + shift) * LOG2E, (EMB, ROWS)).T

    lacc[...] = jnp.zeros_like(lacc)

    def exp_block(b):
        s = dot_nt(uall[me], vall[b])
        e = jnp.exp2(s * LOGIT_SCALE - brow[b])
        exps[b] = e
        part = e[:, 0:128] + e[:, 128:256] + (e[:, 256:384] + e[:, 384:512])
        lacc[...] += part

    exp_block(me)
    gather_pair(vall, (0,), m_vd)
    exp_block(partner)

    def exp_level(masks):
        for m in masks:
            exp_block(dev(m))
        gather_pair(vall, masks, m_vd)
        for m in masks:
            exp_block(dev_other(m))

    gather_level(vall, 0, s_v, m_v, s_vd, m_vd)
    gather_own(uall, s_u, m_u, s_ud, m_ud)

    def exp_pair_loop(level):
        def body(i, _):
            m = LEVELS[level][0] if len(LEVELS[level]) == 1 else (i * (i + 1) // 2 + 1)
            if level == 1:
                m = 7 - m
            exp_block(dev(m))
            return 0
        lax.fori_loop(0, len(LEVELS[level]), body, 0)
        gather_pair(vall, LEVELS[level], m_vd)

        def body2(i, _):
            m = LEVELS[level][0] if len(LEVELS[level]) == 1 else (i * (i + 1) // 2 + 1)
            if level == 1:
                m = 7 - m
            exp_block(dev_other(m))
            return 0
        lax.fori_loop(0, len(LEVELS[level]), body2, 0)

    exp_pair_loop(0)
    gather_level(vall, 1, s_v, m_v, s_vd, m_vd)
    exp_pair_loop(1)
    gather_level(vall, 2, s_v, m_v, s_vd, m_vd)
    gather_level(uall, 0, s_u, m_u, s_ud, m_ud)
    exp_pair_loop(2)

    acc = lacc[...]
    l_row = jnp.sum(acc.T, axis=0, keepdims=True)
    invl[...] = jnp.broadcast_to(1.0 / jnp.sum(acc, axis=1, keepdims=True), (ROWS, EMB))
    pos = (uall[me].astype(F32) * vall[me].astype(F32)).T
    pos_row = jnp.sum(pos, axis=0, keepdims=True)
    loss_row = jnp.log(l_row) + ((shift + lq[...]) - pos_row * (1.0 / TEMPERATURE))
    loss_part = loss_row[:, 0:128] + loss_row[:, 128:256] + (loss_row[:, 256:384] + loss_row[:, 384:512])
    msgs[me, :, 0:ROWS] = 1.0 / l_row
    msgs[me, :, ROWS:MSG] = loss_part

    gather_level(uall, 1, s_u, m_u, s_ud, m_ud)
    for k in range(NDEV - 1):
        send(msgs.at[me], msgs.at[me], s_msg.at[k], m_msg.at[k], others[k])

    eye = (lax.broadcasted_iota(jnp.int32, (ROWS, ROWS), 0)
           == lax.broadcasted_iota(jnp.int32, (ROWS, ROWS), 1))

    def wide(col):
        return jnp.concatenate([col, col, col, col], axis=1)

    g_own = jnp.where(eye, exps[me] * wide(invl[...]) - 1.0, exps[me] * wide(invl[...])).astype(BF16)
    dacc[...] = dot_nn(g_own, vall[me])

    def du_step(i, _):
        b = (me + i) % NDEV
        g = (exps[b] * wide(invl[...])).astype(BF16)
        dacc[...] += dot_nn(g, vall[b])
        return 0
    lax.fori_loop(1, NDEV, du_step, 0)

    gather_level(uall, 2, s_u, m_u, s_ud, m_ud)

    def tower_backward(x, w_out, a_ref, h_ref, u_ref, r_ref, gi, go):
        du = dacc[...] * GRAD_SCALE
        u = u_ref[...]
        de = (r_ref[...] * (du - u * jnp.sum(u * du, axis=-1, keepdims=True))).astype(BF16)
        go[...] = dot_tn(h_ref[...], de)
        dh = dot_nt(de, w_out[...])
        da = jnp.where(a_ref[...] > 0, dh, 0.0).astype(BF16)
        gi[...] = dot_tn(x[...], da)

    def half_in(c):
        return pl.ds(pl.multiple_of(c * 256, 256), 256)

    def half_out(c):
        return pl.ds(pl.multiple_of(c * 128, 128), 128)

    def shard_in(c, k):
        return pl.ds(pl.multiple_of(c * 256 + k * 32, 32), 32)

    def shard_out(c, k):
        return pl.ds(pl.multiple_of(c * 128 + k * 16, 16), 16)

    def pair_start(t, gi, go, pi, po):
        send(gi.at[half_in(1 - core), :], pi, s_pair.at[t, 0], m_pair.at[t, 0], partner)
        send(go.at[half_out(1 - core), :], po, s_pair.at[t, 1], m_pair.at[t, 1], partner)

    def pair_finish(t, gi, go, pi, po, ri, ro):
        arrived(pi, m_pair.at[t, 0])
        arrived(po, m_pair.at[t, 1])
        pi[...] = pi[...] + gi[half_in(core), :]
        po[...] = po[...] + go[half_out(core), :]
        for m in range(7, 0, -1):
            to = dev(m)
            k = to // 2
            send(pi.at[pl.ds(pl.multiple_of(k * 32, 32), 32), :], ri.at[chip], s_rs.at[t, 0, m], m_rs.at[t, 0, m], to)
            send(po.at[pl.ds(pl.multiple_of(k * 16, 16), 16), :], ro.at[chip], s_rs.at[t, 1, m], m_rs.at[t, 1, m], to)

    def rs_finish(t, gi_o, go_o, pi, po, ri, ro, fi, fo):
        for m in range(1, 8):
            k = dev(m) // 2
            arrived(ri.at[k], m_rs.at[t, 0, m])
            arrived(ro.at[k], m_rs.at[t, 1, m])
        ti = pi[pl.ds(pl.multiple_of(chip * 32, 32), 32), :]
        to_ = po[pl.ds(pl.multiple_of(chip * 16, 16), 16), :]
        for m in range(1, 8):
            k = dev(m) // 2
            ti = ti + ri[k]
            to_ = to_ + ro[k]
        gi_o[shard_in(core, chip), :] = ti
        go_o[shard_out(core, chip), :] = to_
        for m in range(7, 0, -1):
            to = dev(m)
            for n, ref in ((0, gi_o.at[shard_in(core, chip), :]), (1, go_o.at[shard_out(core, chip), :])):
                send(ref, ref, s_ag.at[t, n, m], m_ag.at[t, n, m], to)

    def ag_forward(t, gi_o, go_o):
        for m in range(1, 8):
            k = dev(m) // 2
            arrived(gi_o.at[shard_in(core, k), :], m_ag.at[t, 0, m])
            arrived(go_o.at[shard_out(core, k), :], m_ag.at[t, 1, m])
        send(gi_o.at[half_in(core), :], gi_o.at[half_in(core), :], s_fw.at[t, 0], m_fw.at[t, 0], partner)
        send(go_o.at[half_out(core), :], go_o.at[half_out(core), :], s_fw.at[t, 1], m_fw.at[t, 1], partner)

    def ag_finish(t, gi_o, go_o):
        arrived(gi_o.at[half_in(1 - core), :], m_fw.at[t, 0])
        arrived(go_o.at[half_out(1 - core), :], m_fw.at[t, 1])

    def q_part(body):
        return body

    def run(gi_q, go_q, gi_v, go_v):
        tower_backward(qx, wqo, a_q, h_q, u_q, r_q, gi_q, go_q)
        pair_start(0, gi_q, go_q, pi_q, po_q)

        for k in range(NDEV - 1):
            src = (me + NDEV - 1 - k) % NDEV
            arrived(msgs.at[src], m_msg.at[k])
        total = msgs[0, :, ROWS:MSG]
        for b in range(1, NDEV):
            total = total + msgs[b, :, ROWS:MSG]
        loss_out[...] = jnp.broadcast_to(jnp.sum(total, axis=1, keepdims=True) * (1.0 / TOTAL), (1, 128))

        gather_pair(uall, range(8), m_ud)
        pair_finish(0, gi_q, go_q, pi_q, po_q, ri_q, ro_q)

        def dv_block(b, own):
            s = dot_nt(vall[me], uall[b])
            p = jnp.exp2(s * LOGIT_SCALE - wide(bcol[...])) * msgs[b, :, 0:ROWS]
            if own:
                p = jnp.where(eye, p - 1.0, p)
            return dot_nn(p.astype(BF16), uall[b])

        dacc[...] = dv_block(me, True)

        def dv_step(i, _):
            b = (me + i) % NDEV
            dacc[...] += dv_block(b, False)
            return 0
        lax.fori_loop(1, 9, dv_step, 0)
        rs_finish(0, gqi_out, gqo_out, pi_q, po_q, ri_q, ro_q, None, None)
        lax.fori_loop(9, NDEV, dv_step, 0)

        tower_backward(vx, wvo, a_v, h_v, u_v, r_v, gi_v, go_v)
        pair_start(1, gi_v, go_v, pi_v, po_v)
        ag_forward(0, gqi_out, gqo_out)
        pair_finish(1, gi_v, go_v, pi_v, po_v, ri_v, ro_v)
        rs_finish(1, gvi_out, gvo_out, pi_v, po_v, ri_v, ro_v, None, None)
        ag_finish(0, gqi_out, gqo_out)
        ag_forward(1, gvi_out, gvo_out)
        ag_finish(1, gvi_out, gvo_out)
        for copy in pending:
            copy.wait_send()

    pl.run_scoped(run, pltpu.VMEM((FEAT, HID), F32), pltpu.VMEM((HID, EMB), F32),
                  pltpu.VMEM((FEAT, HID), F32), pltpu.VMEM((HID, EMB), F32))


def solution(mesh):
    vmem = pl.BlockSpec(memory_space=pltpu.VMEM)
    dma = pltpu.SemaphoreType.DMA

    def local_step(query_feat, item_feat, log_q, w_query_in, w_query_out, w_item_in, w_item_out):
        shape = jax.ShapeDtypeStruct
        loss, gqi, gqo, gvi, gvo = pl.pallas_call(
            kernel,
            out_shape=(shape((1, 128), F32), shape((FEAT, HID), F32), shape((HID, EMB), F32),
                       shape((FEAT, HID), F32), shape((HID, EMB), F32)),
            in_specs=[vmem] * 7,
            out_specs=(vmem,) * 5,
            scratch_shapes=[
                pltpu.VMEM((NDEV, ROWS, EMB), BF16), pltpu.VMEM((NDEV, ROWS, EMB), BF16),
                pltpu.VMEM((NDEV, 1, ROWS), F32), pltpu.VMEM((NDEV, 1, ROWS), F32),
                pltpu.VMEM((NDEV, 1, MSG), F32),
                pltpu.VMEM((NDEV, ROWS, ROWS), F32), pltpu.VMEM((ROWS, EMB), F32),
                pltpu.VMEM((ROWS, HID), F32), pltpu.VMEM((ROWS, HID), F32),
                pltpu.VMEM((ROWS, HID), BF16), pltpu.VMEM((ROWS, HID), BF16),
                pltpu.VMEM((ROWS, EMB), F32), pltpu.VMEM((ROWS, EMB), F32),
                pltpu.VMEM((ROWS, EMB), F32), pltpu.VMEM((ROWS, EMB), F32),
                pltpu.VMEM((ROWS, EMB), F32), pltpu.VMEM((ROWS, EMB), F32), pltpu.VMEM((ROWS, EMB), F32),
                pltpu.VMEM((256, HID), F32), pltpu.VMEM((128, EMB), F32),
                pltpu.VMEM((256, HID), F32), pltpu.VMEM((128, EMB), F32),
                pltpu.VMEM((8, 32, HID), F32), pltpu.VMEM((8, 16, EMB), F32),
                pltpu.VMEM((8, 32, HID), F32), pltpu.VMEM((8, 16, EMB), F32),
                dma((15,)), dma((15,)), dma((15,)), dma((15,)),
                dma((3, 8, 3)), dma((3, 8)), dma((8,)), dma((8,)),
                dma((3, 8, 3)), dma((3, 8)), dma((8,)), dma((8,)),
                dma((2, 2)), dma((2, 2)), dma((2, 2, 8)), dma((2, 2, 8)),
                dma((2, 2, 8)), dma((2, 2, 8)), dma((2, 2)), dma((2, 2)),
            ],
            compiler_params=pltpu.CompilerParams(collective_id=0, has_side_effects=True,
                                                 vmem_limit_bytes=62 * 1024 * 1024),
            name="step",
        )(query_feat, item_feat, log_q.reshape(1, ROWS), w_query_in, w_query_out, w_item_in, w_item_out)
        return loss[0, 0:1], gqi, gqo, gvi, gvo

    return jax.shard_map(local_step, mesh=mesh, in_specs=(P('dp', None), P('dp', None), P('dp'), P(), P(), P(), P()), out_specs=(P(), P(), P(), P(), P()), check_vma=False)
```

time: 262 us -> 67.8 us (0.26)
  waiting for transfers between devices: 111 us -> 0 us
  Pallas kernels: 0 us -> 60.8 us
  blocking collectives: 46.4 us -> 0 us
  matrix products: 35.2 us -> 0 us
  other arithmetic: 27.9 us -> 0 us
  local copies, waits for them, and re-layouts: 23.8 us -> 4.94 us
  between operations: 15.7 us -> 1.84 us
    pallas_call x0 -> x1, Pallas kernels: none -> 60.8 us  [local_step(): pl.pallas_call(kernel, out_shape=(shape((1, 128), F32), shape((FEAT, HID)...]
    reduce_scatter x1 -> x0, waiting for transfers between devices: 60.2 us -> none  [local_step(): lax.psum_scatter(d_item_part, 'dp', scatter_dimension=0, tiled=True)]
    psum x1 -> x0, waiting for transfers between devices: 37.3 us -> none  [local_step(): lax.psum(grad_query_in, 'dp')]
    dot_general x14 -> x0, matrix products: 35.2 us -> none  [the longest x2 12.6 us: block_step(): jnp.einsum('qk,qe->ke', grad_logits, query_blk, preferred_element_type=jn...]
    psum x1 -> x0, blocking collectives: 31.2 us -> none  [local_step(): loss = jnp.reshape(lax.psum(loss_sum, 'dp') / total_rows, (1,))]
    all_gather x1 -> x0, blocking collectives: 15.1 us -> none  [local_step(): logq_all = lax.all_gather(log_q, 'dp', axis=0, tiled=True)]
    reduce_sum x7 -> x0, other arithmetic: 14.6 us -> none  [the longest x2 11.6 us: block_step(): pos_logit = jnp.sum(jnp.where(is_pos, logits, 0.0), axis=1, keepdims=True)]
    all_gather x1 -> x0, waiting for transfers between devices: 13 us -> none  [local_step(): lax.all_gather(v_unit.astype(jnp.bfloat16), 'dp', axis=0, tiled=True)]
  transfers between devices with their start and end apart: 3 -> 0, of which waited for: 3 -> 0; matrix products, arithmetic and copies ran while one was open for 2% -> 0% of each run, Pallas kernels for 0% -> 0%
where the time goes in v1:
time: 67.8 us; the launch traced here: 67.6 us
  Pallas kernels  60.8 us (90%)
  local copies, waits for them, and re-layouts  4.94 us (7%)
  between operations  1.84 us (3%)
    pallas_call x1, Pallas kernels, local_step(): pl.pallas_call(kernel, out_shape=(shape((1, 128), F32), shape((FEAT, HID)...  60.8 us
    unnamed x12, local copies, waits for them, and re-layouts  4.94 us

profile of v1, /device:TPU:0, one launch (start us, length us, event | category | flops | bytes accessed | tf_op | source)
XLA Modules:
  0.0 67.6 jit_solution(11338635674207251237)
XLA Ops:
  0.6 60.8 %step.1 = (f32[1,128]{1,0:T(1,128)}, f32[512,256]{1,0:T(8,128)}, f32[256,128]{1,0:T(8,128)}, f32[512,256]{1,0:T(8,128)}, f32[256,128]{1,0:T(8,128)}) custom-call(bf16[512,512]{1,0:T(8,128)(2,1)} %qx.1, bf16[512,512]{1,0:T(8,128)(2,1)} %vx.1, f32[1,512]{1,0:T(1,128)} %bitcast.3, bf16[512,256]{1,0:T(8,128)(2,1)} %wqi.1, bf16[256,128]{1,0:T(8,128)(2,1)} %wqo.1, ...), custom_call_target="tpu_custom_call" | custom-call | tf_op jit(solution)/shard_map/step/pallas_call | solution.py:342
  61.5 0.0 copy-start.3
  61.5 0.7 copy-done.3
  62.2 0.0 copy-start.2
  62.2 0.0 copy-start
  62.2 1.9 %copy.18 = f32[512,256]{1,0:T(8,128)} copy(f32[512,256]{1,0:T(8,128)} %get-tuple-element.21) | data formatting | bytes 1048576
  64.1 0.0 copy-done.2
  64.1 0.7 copy.19
  64.8 0.0 copy-done
  64.8 0.0 copy-start.1
  64.8 0.8 %copy.20 = f32[512,256]{1,0:T(8,128)} copy(f32[512,256]{1,0:T(8,128)S(1)} %copy-done) | data formatting | bytes 1048576
  65.6 0.2 copy-done.1
  65.8 0.7 copy.21
Async XLA Ops:
  61.5 0.7 copy-start.3
  62.2 2.0 %copy-start.2 = (f32[256,128]{1,0:T(8,128)S(1)}, f32[256,128]{1,0:T(8,128)}, u32[]{:S(2)}) copy-start(f32[256,128]{1,0:T(8,128)} %get-tuple-element.22) | copy-start | bytes 393220
  62.2 2.6 %copy-start = (f32[512,256]{1,0:T(8,128)S(1)}, f32[512,256]{1,0:T(8,128)}, u32[]{:S(2)}) copy-start(f32[512,256]{1,0:T(8,128)} %get-tuple-element.23) | copy-start | bytes 1572868
  64.8 1.0 %copy-start.1 = (f32[256,128]{1,0:T(8,128)S(1)}, f32[256,128]{1,0:T(8,128)}, u32[]{:S(2)}) copy-start(f32[256,128]{1,0:T(8,128)} %get-tuple-element.24) | copy-start | bytes 393220

commit v2 on v0

v2 whole, which is shorter than its diff:
```python
import jax
import jax.numpy as jnp
from jax import lax
from jax.experimental import pallas as pl
from jax.experimental.pallas import tpu as pltpu
from jax.sharding import PartitionSpec as P

MESH = pl.DeviceIdType.MESH
TEMPERATURE = 0.05
NORM_EPS = 1e-6
LOG2E = 1.4426950408889634
NDEV = 16
ROWS = 512
FEAT = 512
HID = 256
EMB = 128
PACK = FEAT + HID // 2
HALF = PACK // 2
SHARD = HALF // 8
TOTAL = NDEV * ROWS
GRAD_SCALE = 1.0 / (TEMPERATURE * TOTAL)
LOGIT_SCALE = LOG2E / TEMPERATURE
PARTS = ((0, 176), (176, 176), (352, 160))
ORDERS = ((1, 2, 4), (2, 4, 1), (4, 1, 2), (1, 2, 4))
LEVELS = ((1, 2, 4), (6, 5, 3), (7,))
MSG = ROWS + 128
F32 = jnp.float32
BF16 = jnp.bfloat16


def dot_nn(a, b):
    return lax.dot_general(a, b, (((1,), (0,)), ((), ())), preferred_element_type=F32)


def dot_nt(a, b):
    return lax.dot_general(a, b, (((1,), (1,)), ((), ())), preferred_element_type=F32)


def dot_tn(a, b):
    return lax.dot_general(a, b, (((0,), (0,)), ((), ())), preferred_element_type=F32)


def wide(col):
    return jnp.concatenate([col, col, col, col], axis=1)


def kernel(qx_h, vx_h, lq_h, wqi_h, wqo_h, wvi_h, wvo_h,
           loss_out, gq_out, gv_out,
           qx, vx, wqi, wqo, wvi, wvo, s_in,
           uall, vall, lqall, cmax, crun, msgs, exps, lacc,
           a_q, a_v, h_q, h_v, u_q, u_v, r_q, r_v, invl, bcol, dacc,
           gp_q, gp_v, pp_q, pp_v, rr_q, rr_v,
           s_msg, m_msg,
           s_v, m_v, s_vd, m_vd, s_ld, m_ld, s_u, m_u, s_ud, m_ud,
           s_pair, m_pair, s_rs, m_rs, s_ag, m_ag, s_fw, m_fw):
    me = lax.axis_index("dp")
    core = me % 2
    bit_x, bit_y, bit_z = (me // 2) % 2, (me // 4) % 2, (me // 8) % 2
    step_x, step_y, step_z = 2 - 4 * bit_x, 4 - 8 * bit_y, 8 - 16 * bit_z
    partner = me + 1 - 2 * core
    chip = me // 2

    def dev(mask):
        return me + (mask % 2) * step_x + ((mask // 2) % 2) * step_y + (mask // 4) * step_z

    def dev_other(mask):
        return partner + (mask % 2) * step_x + ((mask // 2) % 2) * step_y + (mask // 4) * step_z

    def rcopy(src, dst, ssem, rsem, to):
        return pltpu.make_async_remote_copy(src_ref=src, dst_ref=dst, send_sem=ssem, recv_sem=rsem,
                                            device_id=(to,), device_id_type=MESH)

    pending = []

    def send(src, dst, ssem, rsem, to):
        copy = rcopy(src, dst, ssem, rsem, to)
        copy.start()
        pending.append(copy)

    def arrived(ref, rsem):
        rcopy(ref, ref, rsem, rsem, partner).wait_recv()

    others = [(me + k) % NDEV for k in range(1, NDEV)]

    loads = [pltpu.make_async_copy(src, dst, s_in.at[i]) for i, (src, dst) in enumerate((
        (vx_h, vx), (wvi_h, wvi), (wvo_h, wvo), (lq_h, lqall.at[me]), (qx_h, qx), (wqi_h, wqi), (wqo_h, wqo)))]
    for load in loads:
        load.start()
    barrier = pltpu.get_barrier_semaphore()
    for to in (partner, dev(1), dev(2), dev(4)):
        pl.semaphore_signal(barrier, inc=1, device_id=(to,), device_id_type=MESH)

    def tower_forward(x, w_in, w_out, a_ref, h_ref, u_ref, r_ref, all_ref):
        a = dot_nn(x[...], w_in[...])
        a_ref[...] = a
        h = jnp.maximum(a, 0.0).astype(BF16)
        h_ref[...] = h
        e = dot_nn(h, w_out[...])
        r = lax.rsqrt(jnp.sum(e * e, axis=-1, keepdims=True) + NORM_EPS)
        u = e * r
        u_ref[...] = u
        r_ref[...] = jnp.broadcast_to(r, (ROWS, EMB))
        all_ref[me] = u.astype(BF16)

    for load in loads[:4]:
        load.wait()
    tower_forward(vx, wvi, wvo, a_v, h_v, u_v, r_v, vall)
    pl.semaphore_wait(barrier, 4)

    def part_ref(ref, src, p):
        if p == 3:
            return lqall.at[src]
        return ref.at[src, pl.ds(PARTS[p][0], PARTS[p][1]), :]

    def send_part(ref, src, p, m, t, ss, ms):
        d = ORDERS[p][t]
        send(part_ref(ref, src, p), part_ref(ref, src, p), ss.at[p, m, t], ms.at[p, m + d], dev(d))

    def gather_own(ref, ts, ps, ss, ms):
        for t in ts:
            for p in ps:
                send_part(ref, me, p, 0, t, ss, ms)

    def level_jobs(level, ps):
        jobs = []
        for p in ps:
            for m in LEVELS[level]:
                top = max(t for t in range(3) if ORDERS[p][t] & m)
                jobs.append((top, p, m))
        return sorted(jobs)

    def gather_jobs(ref, jobs, ss, ms):
        for top, p, m in jobs:
            src = dev(m)
            arrived(part_ref(ref, src, p), ms.at[p, m])
            for t in range(top + 1, 3):
                send_part(ref, src, p, m, t, ss, ms)

    def pair_send(ref, masks, sd, md):
        for m in masks:
            send(ref.at[dev(m)], ref.at[dev(m)], sd.at[m], md.at[m], partner)

    def pair_wait(ref, masks, md):
        for m in masks:
            arrived(ref.at[dev_other(m)], md.at[m])

    VP, UP = (3, 0, 1, 2), (0, 1, 2)
    pair_send(lqall, (0,), s_ld, m_ld)
    pair_send(vall, (0,), s_vd, m_vd)
    gather_own(vall, (0, 1, 2), VP, s_v, m_v)

    for load in loads[4:]:
        load.wait()
    tower_forward(qx, wqi, wqo, a_q, h_q, u_q, r_q, uall)
    pair_send(uall, (0,), s_ud, m_ud)

    crun[...] = jnp.broadcast_to(jnp.max(-lqall[me], axis=1, keepdims=True), (1, 128))
    lacc[...] = jnp.zeros_like(lacc)

    def exp_block(b):
        lq_b = lqall[b]
        c_b = jnp.max(-lq_b, axis=1, keepdims=True)
        cmax[b] = jnp.broadcast_to(c_b, (1, 128))
        s = dot_nt(uall[me], vall[b])
        e = jnp.exp2(s * LOGIT_SCALE - (lq_b + c_b) * LOG2E)
        exps[b] = e
        part = e[:, 0:128] + e[:, 128:256] + (e[:, 256:384] + e[:, 384:512])
        c_old = crun[...]
        c_new = jnp.maximum(c_old, cmax[b])
        lacc[...] = lacc[...] * jnp.exp2((c_old - c_new) * LOG2E) + part * jnp.exp2((cmax[b] - c_new) * LOG2E)
        crun[...] = c_new

    exp_block(me)
    pair_wait(lqall, (0,), m_ld)
    pair_wait(vall, (0,), m_vd)
    exp_block(partner)

    L0, L1, L2 = LEVELS
    gather_jobs(vall, level_jobs(0, VP), s_v, m_v)
    gather_own(uall, (0,), UP, s_u, m_u)
    pair_send(lqall, L0, s_ld, m_ld)
    pair_send(vall, L0, s_vd, m_vd)
    for m in L0:
        exp_block(dev(m))
    gather_jobs(vall, level_jobs(1, VP), s_v, m_v)
    gather_own(uall, (1, 2), UP, s_u, m_u)
    pair_send(lqall, L1, s_ld, m_ld)
    pair_send(vall, L1, s_vd, m_vd)
    pair_wait(lqall, L0, m_ld)
    pair_wait(vall, L0, m_vd)
    for m in L0:
        exp_block(dev_other(m))
    u_jobs = level_jobs(0, UP)
    gather_jobs(uall, u_jobs[:3], s_u, m_u)
    for m in L1:
        exp_block(dev(m))
    gather_jobs(vall, level_jobs(2, VP), s_v, m_v)
    pair_send(lqall, L2, s_ld, m_ld)
    pair_send(vall, L2, s_vd, m_vd)
    gather_jobs(uall, u_jobs[3:], s_u, m_u)
    pair_send(uall, L0, s_ud, m_ud)
    pair_wait(lqall, L1, m_ld)
    pair_wait(vall, L1, m_vd)
    for m in L1:
        exp_block(dev_other(m))
    exp_block(dev(7))
    pair_wait(lqall, L2, m_ld)
    pair_wait(vall, L2, m_vd)
    exp_block(dev_other(7))

    acc = lacc[...]
    shift = crun[0:1, 0:1]
    lq_own = lqall[me]
    l_row = jnp.sum(acc.T, axis=0, keepdims=True)
    pos = (uall[me].astype(F32) * vall[me].astype(F32)).T
    pos_row = jnp.sum(pos, axis=0, keepdims=True)
    loss_row = jnp.log(l_row) + ((shift + lq_own) - pos_row * (1.0 / TEMPERATURE))
    loss_part = loss_row[:, 0:128] + loss_row[:, 128:256] + (loss_row[:, 256:384] + loss_row[:, 384:512])
    msgs[me, :, 0:ROWS] = 1.0 / l_row
    msgs[me, :, ROWS:MSG] = loss_part
    gather_jobs(uall, level_jobs(1, UP), s_u, m_u)
    pair_send(uall, L1, s_ud, m_ud)
    for k in range(NDEV - 1):
        send(msgs.at[me], msgs.at[me], s_msg.at[k], m_msg.at[k], others[k])
    invl[...] = jnp.broadcast_to(1.0 / jnp.sum(acc, axis=1, keepdims=True), (ROWS, EMB))
    bcol[...] = jnp.broadcast_to((lq_own + shift) * LOG2E, (EMB, ROWS)).T

    eye = (lax.broadcasted_iota(jnp.int32, (ROWS, ROWS), 0)
           == lax.broadcasted_iota(jnp.int32, (ROWS, ROWS), 1))

    def prob_block(b):
        return exps[b] * wide(invl[...] * jnp.exp2((cmax[b] - crun[...]) * LOG2E))

    p_own = prob_block(me)
    dacc[...] = dot_nn(jnp.where(eye, p_own - 1.0, p_own).astype(BF16), vall[me])

    def du_step(i, _):
        total = dacc[...]
        for j in range(3):
            b = (me + 3 * i + j + 1) % NDEV
            total = total + dot_nn(prob_block(b).astype(BF16), vall[b])
        dacc[...] = total
        return 0
    lax.fori_loop(0, 3, du_step, 0)
    gather_jobs(uall, level_jobs(2, UP), s_u, m_u)
    pair_send(uall, L2, s_ud, m_ud)
    lax.fori_loop(3, 5, du_step, 0)

    def tower_backward(x, w_out, a_ref, h_ref, u_ref, r_ref, g):
        du = dacc[...] * GRAD_SCALE
        u = u_ref[...]
        de = (r_ref[...] * (du - u * jnp.sum(u * du, axis=-1, keepdims=True))).astype(BF16)
        go = dot_tn(h_ref[...], de)
        g[FEAT:PACK, 0:EMB] = go[0:128]
        g[FEAT:PACK, EMB:HID] = go[128:256]
        dh = dot_nt(de, w_out[...])
        da = jnp.where(a_ref[...] > 0, dh, 0.0).astype(BF16)
        g[0:FEAT, :] = dot_tn(x[...], da)

    def half(c):
        return pl.ds(pl.multiple_of(c * HALF, 8), HALF)

    def shard(c, k):
        return pl.ds(pl.multiple_of(c * HALF + k * SHARD, 8), SHARD)

    NEAR = (1, 2, 4, 3, 5, 6, 7)

    def pair_start(t, g, pp):
        send(g.at[half(1 - core), :], pp, s_pair.at[t], m_pair.at[t], partner)

    def pair_finish(t, g, pp, rr):
        arrived(pp, m_pair.at[t])
        pp[...] = pp[...] + g[half(core), :]
        for m in reversed(NEAR):
            to = dev(m)
            k = to // 2
            send(pp.at[pl.ds(pl.multiple_of(k * SHARD, 8), SHARD), :], rr.at[chip], s_rs.at[t, m], m_rs.at[t, m], to)

    def rs_finish(t, out, pp, rr):
        total = pp[pl.ds(pl.multiple_of(chip * SHARD, 8), SHARD), :]
        for m in NEAR:
            k = dev(m) // 2
            arrived(rr.at[k], m_rs.at[t, m])
            total = total + rr[k]
        out[shard(core, chip), :] = total
        ref = out.at[shard(core, chip), :]
        for m in reversed(NEAR):
            send(ref, ref, s_ag.at[t, m], m_ag.at[t, m], dev(m))
        send(ref, ref, s_fw.at[t, 0], m_fw.at[t, 0], partner)

    def ag_forward(t, out):
        for m in NEAR:
            ref = out.at[shard(core, dev(m) // 2), :]
            arrived(ref, m_ag.at[t, m])
            send(ref, ref, s_fw.at[t, m], m_fw.at[t, m], partner)

    def ag_finish(t, out):
        for m in (0,) + NEAR:
            arrived(out.at[shard(1 - core, dev(m) // 2), :], m_fw.at[t, m])

    tower_backward(qx, wqo, a_q, h_q, u_q, r_q, gp_q)
    pair_start(0, gp_q, pp_q)

    for k in range(NDEV - 1):
        src = (me + NDEV - 1 - k) % NDEV
        arrived(msgs.at[src], m_msg.at[k])
    total = msgs[0, :, ROWS:MSG]
    for b in range(1, NDEV):
        total = total + msgs[b, :, ROWS:MSG]
    loss_out[...] = jnp.broadcast_to(jnp.sum(total, axis=1, keepdims=True) * (1.0 / TOTAL), (1, 128))

    def dv_block(b, own):
        s = dot_nt(vall[me], uall[b])
        p = jnp.exp2(s * LOGIT_SCALE - wide(bcol[...])) * msgs[b, :, 0:ROWS]
        if own:
            p = jnp.where(eye, p - 1.0, p)
        return dot_nn(p.astype(BF16), uall[b])

    dacc[...] = dv_block(me, True)
    pair_finish(0, gp_q, pp_q, rr_q)
    pair_wait(uall, (0,) + NEAR, m_ud)

    def dv_step(i, _):
        total = dacc[...]
        for j in range(3):
            total = total + dv_block((me + 3 * i + j + 1) % NDEV, False)
        dacc[...] = total
        return 0
    lax.fori_loop(0, 3, dv_step, 0)
    rs_finish(0, gq_out, pp_q, rr_q)
    lax.fori_loop(3, 5, dv_step, 0)

    tower_backward(vx, wvo, a_v, h_v, u_v, r_v, gp_v)
    pair_start(1, gp_v, pp_v)
    ag_forward(0, gq_out)
    pair_finish(1, gp_v, pp_v, rr_v)
    ag_finish(0, gq_out)
    rs_finish(1, gv_out, pp_v, rr_v)
    ag_forward(1, gv_out)
    ag_finish(1, gv_out)
    for copy in pending:
        copy.wait_send()


def finish(loss, gq, gv, loss_out, gqi, gqo, gvi, gvo, sem):
    copies = []
    for i, (g, gi, go) in enumerate(((gq, gqi, gqo), (gv, gvi, gvo))):
        copies.append(pltpu.make_async_copy(g.at[0:FEAT, :], gi, sem.at[i, 0]))
        copies.append(pltpu.make_async_copy(g.at[FEAT:PACK, 0:EMB], go.at[0:128, :], sem.at[i, 1]))
        copies.append(pltpu.make_async_copy(g.at[FEAT:PACK, EMB:HID], go.at[128:256, :], sem.at[i, 2]))
    for copy in copies:
        copy.start()
    loss_out[0] = loss[0, 0]
    for copy in copies:
        copy.wait()


def solution(mesh):
    vmem = pl.BlockSpec(memory_space=pltpu.VMEM)
    smem = pl.BlockSpec(memory_space=pltpu.SMEM)
    hbm = pl.BlockSpec(memory_space=pltpu.HBM)
    anym = pl.BlockSpec(memory_space=pl.ANY)
    dma = pltpu.SemaphoreType.DMA
    V = pltpu.VMEM

    def local_step(query_feat, item_feat, log_q, w_query_in, w_query_out, w_item_in, w_item_out):
        shape = jax.ShapeDtypeStruct
        loss, gq, gv = pl.pallas_call(
            kernel,
            out_shape=(shape((1, 128), F32), shape((PACK, HID), F32), shape((PACK, HID), F32)),
            in_specs=[hbm] * 7,
            out_specs=(vmem, vmem, vmem),
            scratch_shapes=[
                V((ROWS, FEAT), BF16), V((ROWS, FEAT), BF16),
                V((FEAT, HID), BF16), V((HID, EMB), BF16), V((FEAT, HID), BF16), V((HID, EMB), BF16), dma((7,)),
                V((NDEV, ROWS, EMB), BF16), V((NDEV, ROWS, EMB), BF16),
                V((NDEV, 1, ROWS), F32), V((NDEV, 1, 128), F32), V((1, 128), F32),
                V((NDEV, 1, MSG), F32),
                V((NDEV, ROWS, ROWS), F32), V((ROWS, EMB), F32),
                V((ROWS, HID), F32), V((ROWS, HID), F32),
                V((ROWS, HID), BF16), V((ROWS, HID), BF16),
                V((ROWS, EMB), F32), V((ROWS, EMB), F32),
                V((ROWS, EMB), F32), V((ROWS, EMB), F32),
                V((ROWS, EMB), F32), V((ROWS, EMB), F32), V((ROWS, EMB), F32),
                V((PACK, HID), F32), V((PACK, HID), F32),
                V((HALF, HID), F32), V((HALF, HID), F32),
                V((8, SHARD, HID), F32), V((8, SHARD, HID), F32),
                dma((15,)), dma((15,)),
                dma((4, 8, 3)), dma((4, 8)), dma((8,)), dma((8,)), dma((8,)), dma((8,)),
                dma((3, 8, 3)), dma((3, 8)), dma((8,)), dma((8,)),
                dma((2,)), dma((2,)), dma((2, 8)), dma((2, 8)),
                dma((2, 8)), dma((2, 8)), dma((2, 8)), dma((2, 8)),
            ],
            compiler_params=pltpu.CompilerParams(collective_id=0, has_side_effects=True,
                                                 vmem_limit_bytes=48 * 1024 * 1024),
            name="step",
        )(*(pltpu.with_memory_space_constraint(x, pltpu.HBM) for x in (
            query_feat, item_feat, log_q.reshape(1, ROWS), w_query_in, w_query_out, w_item_in, w_item_out)))
        return pl.pallas_call(
            finish,
            out_shape=(shape((1,), F32), shape((FEAT, HID), F32), shape((HID, EMB), F32),
                       shape((FEAT, HID), F32), shape((HID, EMB), F32)),
            in_specs=[vmem, vmem, vmem],
            out_specs=(smem, hbm, hbm, hbm, hbm),
            scratch_shapes=[dma((2, 3))],
            compiler_params=pltpu.CompilerParams(vmem_limit_bytes=8 * 1024 * 1024),
            name="finish",
        )(loss, gq, gv)

    return jax.shard_map(local_step, mesh=mesh, in_specs=(P('dp', None), P('dp', None), P('dp'), P(), P(), P(), P()), out_specs=(P(), P(), P(), P(), P()), check_vma=False)
```

time: 262 us -> 55.7 us (0.21)
  waiting for transfers between devices: 111 us -> 0 us
  Pallas kernels: 0 us -> 54.9 us
  blocking collectives: 46.4 us -> 0 us
  matrix products: 35.2 us -> 0 us
  other arithmetic: 27.9 us -> 0 us
  local copies, waits for them, and re-layouts: 23.8 us -> 0 us
  between operations: 15.7 us -> 0.64 us
    reduce_scatter x1 -> x0, waiting for transfers between devices: 60.2 us -> none  [local_step(): lax.psum_scatter(d_item_part, 'dp', scatter_dimension=0, tiled=True)]
    pallas_call x0 -> x2, Pallas kernels: none -> 54.9 us  [the longest x1 53.3 us: local_step(): pl.pallas_call(kernel, out_shape=(shape((1, 128), F32), shape((PACK, HID)...]
    psum x1 -> x0, waiting for transfers between devices: 37.3 us -> none  [local_step(): lax.psum(grad_query_in, 'dp')]
    dot_general x14 -> x0, matrix products: 35.2 us -> none  [the longest x2 12.6 us: block_step(): jnp.einsum('qk,qe->ke', grad_logits, query_blk, preferred_element_type=jn...]
    psum x1 -> x0, blocking collectives: 31.2 us -> none  [local_step(): loss = jnp.reshape(lax.psum(loss_sum, 'dp') / total_rows, (1,))]
    all_gather x1 -> x0, blocking collectives: 15.1 us -> none  [local_step(): logq_all = lax.all_gather(log_q, 'dp', axis=0, tiled=True)]
    reduce_sum x7 -> x0, other arithmetic: 14.6 us -> none  [the longest x2 11.6 us: block_step(): pos_logit = jnp.sum(jnp.where(is_pos, logits, 0.0), axis=1, keepdims=True)]
    all_gather x1 -> x0, waiting for transfers between devices: 13 us -> none  [local_step(): lax.all_gather(v_unit.astype(jnp.bfloat16), 'dp', axis=0, tiled=True)]
  transfers between devices with their start and end apart: 3 -> 0, of which waited for: 3 -> 0; matrix products, arithmetic and copies ran while one was open for 2% -> 0% of each run, Pallas kernels for 0% -> 0%
where the time goes in v2:
time: 55.7 us; the launch traced here: 55.6 us
  Pallas kernels  54.9 us (99%)
  between operations  0.64 us (1%)
    pallas_call x1, Pallas kernels, local_step(): pl.pallas_call(kernel, out_shape=(shape((1, 128), F32), shape((PACK, HID)...  53.3 us
    pallas_call x1, Pallas kernels, local_step(): pl.pallas_call(finish, out_shape=(shape((1,), F32), shape((FEAT, HID), F3...  1.61 us

profile of v2, /device:TPU:0, one launch (start us, length us, event | category | flops | bytes accessed | tf_op | source)
XLA Modules:
  0.0 55.6 jit_solution(4288237985265906905)
XLA Ops:
  0.6 53.3 %step.1 = (f32[1,128]{1,0:T(1,128)S(1)}, f32[640,256]{1,0:T(8,128)S(1)}, f32[640,256]{1,0:T(8,128)S(1)}) custom-call(bf16[512,512]{1,0:T(8,128)(2,1)} %qx_h.1, bf16[512,512]{1,0:T(8,128)(2,1)} %vx_h.1, f32[1,512]{1,0:T(1,128)} %bitcast.1, bf16[512,256]{1,0:T(8,128)(2,1)} %wqi_h.1, bf16[256,128]{1,0:T(8,128)(2,1)} %wqo_h.1, bf16[512,256]{1,0:T(8,128)(2,1)} %wvi_h.1, ...), custom_call_target="tpu_custom_call" | custom-call | tf_op jit(solution)/shard_map/step/pallas_call | solution.py:368
  53.9 1.6 %finish.1 = (f32[1]{0:T(128)}, f32[512,256]{1,0:T(8,128)}, f32[256,128]{1,0:T(8,128)}, f32[512,256]{1,0:T(8,128)}, f32[256,128]{1,0:T(8,128)}) custom-call(f32[1,128]{1,0:T(1,128)S(1)} %get-tuple-element.8.loss, f32[640,256]{1,0:T(8,128)S(1)} %get-tuple-element.9.gq, f32[640,256]{1,0:T(8,128)S(1)} %get-tuple-element.10.gv), custom_call_target="tpu_custom_call" | custom-call | tf_op jit(solution)/shard_map/finish/pallas_call | solution.py:399

commit v3 on v2

v3 whole, which is shorter than its diff:
```python
import jax
import jax.numpy as jnp
from jax import lax
from jax.experimental import pallas as pl
from jax.experimental.pallas import tpu as pltpu
from jax.sharding import PartitionSpec as P

MESH = pl.DeviceIdType.MESH
TEMPERATURE = 0.05
NORM_EPS = 1e-6
LOG2E = 1.4426950408889634
NDEV = 16
ROWS = 512
FEAT = 512
HID = 256
EMB = 128
PACK = 2 * FEAT + HID
HALF = PACK // 2
SUM_BASE = (0, 192, 384)
SUM_ROWS = (192, 192, 256)
TOTAL = NDEV * ROWS
GRAD_SCALE = 1.0 / (TEMPERATURE * TOTAL)
LOGIT_SCALE = LOG2E / TEMPERATURE
PARTS = ((0, 176), (176, 176), (352, 160))
ORDERS = ((1, 2, 4), (2, 4, 1), (4, 1, 2), (1, 2, 4))
LEVELS = ((1, 2, 4), (6, 5, 3), (7,))
MSG = ROWS + 128
F32 = jnp.float32
BF16 = jnp.bfloat16


def dot_nn(a, b):
    return lax.dot_general(a, b, (((1,), (0,)), ((), ())), preferred_element_type=F32)


def dot_nt(a, b):
    return lax.dot_general(a, b, (((1,), (1,)), ((), ())), preferred_element_type=F32)


def dot_tn(a, b):
    return lax.dot_general(a, b, (((0,), (0,)), ((), ())), preferred_element_type=F32)


def wide(col):
    return jnp.concatenate([col, col, col, col], axis=1)


def kernel(qx_h, vx_h, lq_h, wqi_h, wqo_h, wvi_h, wvo_h,
           loss_out, gq_out, gv_out,
           qx, vx, wqi, wqo, wvi, wvo, s_in,
           uall, vall, lqall, crun, msgs, lacc, diag,
           a_q, a_v, h_q, h_v, u_q, u_v, r_q, r_v, invl, bcol, dacc,
           gp_q, gp_v, pp_q, pp_v, ra_q, ra_v, rb_q, rb_v,
           s_msg, m_msg,
           s_v, m_v, s_vd, m_vd, s_ld, m_ld, s_u, m_u, s_ud, m_ud,
           s_pair, m_pair, s_r1, m_r1, s_r2, m_r2, s_g1, m_g1, s_g2, m_g2, s_fw, m_fw):
    me = lax.axis_index("dp")
    core = me % 2
    bit_x, bit_y, bit_z = (me // 2) % 2, (me // 4) % 2, (me // 8) % 2
    step_x, step_y, step_z = 2 - 4 * bit_x, 4 - 8 * bit_y, 8 - 16 * bit_z
    partner = me + 1 - 2 * core
    chip = me // 2

    def dev(mask):
        return me + (mask % 2) * step_x + ((mask // 2) % 2) * step_y + (mask // 4) * step_z

    def dev_other(mask):
        return partner + (mask % 2) * step_x + ((mask // 2) % 2) * step_y + (mask // 4) * step_z

    def rcopy(src, dst, ssem, rsem, to):
        return pltpu.make_async_remote_copy(src_ref=src, dst_ref=dst, send_sem=ssem, recv_sem=rsem,
                                            device_id=(to,), device_id_type=MESH)

    pending = []

    def send(make):
        rcopy(*make()).start()
        pending.append(make)

    def arrived(ref, rsem):
        rcopy(ref, ref, rsem, rsem, partner).wait_recv()

    others = [(me + k) % NDEV for k in range(1, NDEV)]

    loads = [pltpu.make_async_copy(src, dst, s_in.at[i]) for i, (src, dst) in enumerate((
        (vx_h, vx), (wvi_h, wvi), (wvo_h, wvo), (lq_h, lqall.at[me]), (qx_h, qx), (wqi_h, wqi), (wqo_h, wqo)))]
    for load in loads:
        load.start()
    barrier = pltpu.get_barrier_semaphore()
    for to in (partner, dev(1), dev(2), dev(4)):
        pl.semaphore_signal(barrier, inc=1, device_id=(to,), device_id_type=MESH)

    def tower_forward(x, w_in, w_out, a_ref, h_ref, u_ref, r_ref, all_ref):
        a = dot_nn(x[...], w_in[...])
        a_ref[...] = a
        h = jnp.maximum(a, 0.0).astype(BF16)
        h_ref[...] = h
        e = dot_nn(h, w_out[...])
        r = lax.rsqrt(jnp.sum(e * e, axis=-1, keepdims=True) + NORM_EPS)
        u = e * r
        u_ref[...] = u
        r_ref[...] = jnp.broadcast_to(r, (ROWS, EMB))
        all_ref[me] = u.astype(BF16)

    for load in loads[:4]:
        load.wait()
    tower_forward(vx, wvi, wvo, a_v, h_v, u_v, r_v, vall)
    pl.semaphore_wait(barrier, 4)

    def part_ref(ref, src, p):
        if p == 3:
            return lqall.at[src]
        return ref.at[src, pl.ds(PARTS[p][0], PARTS[p][1]), :]

    def send_part(ref, p, m, t, ss, ms):
        d = ORDERS[p][t]
        send(lambda: (part_ref(ref, dev(m), p), part_ref(ref, dev(m), p), ss.at[p, m, t], ms.at[p, m + d], dev(d)))

    def gather_own(ref, ts, ps, ss, ms):
        for t in ts:
            for p in ps:
                send_part(ref, p, 0, t, ss, ms)

    def level_jobs(level, ps):
        jobs = []
        for p in ps:
            for m in LEVELS[level]:
                top = max(t for t in range(3) if ORDERS[p][t] & m)
                jobs.append((top, p, m))
        return sorted(jobs)

    def gather_jobs(ref, jobs, ss, ms):
        for top, p, m in jobs:
            src = dev(m)
            arrived(part_ref(ref, src, p), ms.at[p, m])
            for t in range(top + 1, 3):
                send_part(ref, p, m, t, ss, ms)

    def pair_send(ref, masks, sd, md):
        for m in masks:
            send(lambda m=m: (ref.at[dev(m)], ref.at[dev(m)], sd.at[m], md.at[m], partner))

    def pair_wait(ref, masks, md):
        for m in masks:
            arrived(ref.at[dev_other(m)], md.at[m])

    VP, UP = (3, 0, 1, 2), (0, 1, 2)
    pair_send(lqall, (0,), s_ld, m_ld)
    pair_send(vall, (0,), s_vd, m_vd)
    gather_own(vall, (0, 1, 2), VP, s_v, m_v)

    for load in loads[4:]:
        load.wait()
    tower_forward(qx, wqi, wqo, a_q, h_q, u_q, r_q, uall)
    pair_send(uall, (0,), s_ud, m_ud)

    eye = (lax.broadcasted_iota(jnp.int32, (ROWS, ROWS), 0)
           == lax.broadcasted_iota(jnp.int32, (ROWS, ROWS), 1))

    def block_shift(b):
        return jnp.max(-lqall[b], axis=1, keepdims=True)

    def exp_block(b, c):
        s = dot_nt(uall[me], vall[b])
        return jnp.exp2(s * LOGIT_SCALE - (lqall[b] + c) * LOG2E)

    def lane_sum(e):
        return e[:, 0:128] + e[:, 128:256] + (e[:, 256:384] + e[:, 384:512])

    def exp_group(blocks):
        c_old = crun[...]
        c = c_old
        for b in blocks:
            c = jnp.maximum(c, block_shift(b))
        crun[...] = c
        scale = jnp.exp2((c_old - c) * LOG2E)
        l_new, d_new = lacc[...] * scale, dacc[...] * scale
        for b in blocks:
            e = exp_block(b, c[:, 0:1])
            l_new = l_new + lane_sum(e)
            d_new = d_new + dot_nn(e.astype(BF16), vall[b])
        lacc[...], dacc[...] = l_new, d_new

    c_own = block_shift(me)
    crun[...] = jnp.broadcast_to(c_own, (1, 128))
    e_own = exp_block(me, c_own)
    lacc[...] = lane_sum(e_own)
    diag[...] = jnp.broadcast_to(jnp.sum(jnp.where(eye, e_own, 0.0), axis=1, keepdims=True), (ROWS, EMB))
    dacc[...] = dot_nn(jnp.where(eye, 0.0, e_own).astype(BF16), vall[me])
    pair_wait(lqall, (0,), m_ld)
    pair_wait(vall, (0,), m_vd)
    exp_group((partner,))

    L0, L1, L2 = LEVELS
    v0, v1, v2 = (level_jobs(k, VP) for k in range(3))
    u0, u1, u2 = (level_jobs(k, UP) for k in range(3))

    def group_devs(g):
        masks = [b + (g // 2) * (7 - 2 * b) for b in L0]
        return [dev(m) + (g % 2) * (partner - me) for m in masks]

    def exp_step(g, _):
        @pl.when(g == 0)
        def _():
            gather_jobs(vall, v0, s_v, m_v)
            pair_send(lqall, L0, s_ld, m_ld)
            pair_send(vall, L0, s_vd, m_vd)

        @pl.when(g == 1)
        def _():
            gather_jobs(vall, v1[:4], s_v, m_v)
            gather_own(uall, (0, 1, 2), UP, s_u, m_u)
            pair_wait(lqall, L0, m_ld)
            pair_wait(vall, L0, m_vd)

        @pl.when(g == 2)
        def _():
            gather_jobs(vall, v1[4:], s_v, m_v)
            pair_send(lqall, L1, s_ld, m_ld)
            pair_send(vall, L1, s_vd, m_vd)

        @pl.when(g == 3)
        def _():
            gather_jobs(vall, v2, s_v, m_v)
            pair_send(lqall, L2, s_ld, m_ld)
            pair_send(vall, L2, s_vd, m_vd)
            pair_wait(lqall, L1, m_ld)
            pair_wait(vall, L1, m_vd)

        exp_group(group_devs(g))
        return 0

    lax.fori_loop(0, 4, exp_step, 0)
    gather_jobs(uall, u0[:3], s_u, m_u)
    pair_wait(lqall, L2, m_ld)
    pair_wait(vall, L2, m_vd)
    exp_group((dev(7), dev_other(7)))

    acc = lacc[...]
    shift = crun[0:1, 0:1]
    lq_own = lqall[me]
    l_row = jnp.sum(acc.T, axis=0, keepdims=True)
    pos = (uall[me].astype(F32) * vall[me].astype(F32)).T
    pos_row = jnp.sum(pos, axis=0, keepdims=True)
    loss_row = jnp.log(l_row) + ((shift + lq_own) - pos_row * (1.0 / TEMPERATURE))
    loss_part = loss_row[:, 0:128] + loss_row[:, 128:256] + (loss_row[:, 256:384] + loss_row[:, 384:512])
    msgs[me, :, 0:ROWS] = 1.0 / l_row
    msgs[me, :, ROWS:MSG] = loss_part
    for k in range(NDEV - 1):
        send(lambda k=k: (msgs.at[me], msgs.at[me], s_msg.at[k], m_msg.at[k], others[k]))
    invl[...] = jnp.broadcast_to(1.0 / jnp.sum(acc, axis=1, keepdims=True), (ROWS, EMB))
    bcol[...] = jnp.broadcast_to((lq_own + shift) * LOG2E, (EMB, ROWS)).T

    p_own = diag[...] * jnp.exp2((c_own - crun[...]) * LOG2E) * invl[...]
    dacc[...] = dacc[...] * invl[...] + (p_own - 1.0).astype(BF16).astype(F32) * vall[me].astype(F32)
    gather_jobs(uall, u0[3:6], s_u, m_u)

    def tower_backward(x, w_out, a_ref, h_ref, u_ref, r_ref, g):
        du = dacc[...] * GRAD_SCALE
        u = u_ref[...]
        de = (r_ref[...] * (du - u * jnp.sum(u * du, axis=-1, keepdims=True))).astype(BF16)
        g[2 * FEAT:PACK, :] = dot_tn(h_ref[...], de)
        dh = dot_nt(de, w_out[...])
        da = jnp.where(a_ref[...] > 0, dh, 0.0).astype(BF16)
        gi = dot_tn(x[...], da)
        g[0:FEAT, :] = gi[:, 0:EMB]
        g[FEAT:2 * FEAT, :] = gi[:, EMB:HID]

    bit = {1: bit_x, 2: bit_y, 4: bit_z}
    PLANE = ((0, 1), (1, 0), (1, 1))

    def rows(base, size):
        return pl.ds(pl.multiple_of(base, 8), size)

    def slot(p, b0, b1, b2, count):
        eighth = SUM_ROWS[p] // 8
        return rows(SUM_BASE[p] + (b0 * 4 + b1 * 2 + b2) * eighth, count * eighth)

    def half(c):
        return rows(c * HALF, HALF)

    def out_slot(c, p, b0, b1, b2, count):
        eighth = SUM_ROWS[p] // 8
        return rows(c * HALF + SUM_BASE[p] + (b0 * 4 + b1 * 2 + b2) * eighth, count * eighth)

    def bits(p, f1=0, f2=0):
        d0, d1, d2 = ORDERS[p]
        b1 = bit[d1] if not f1 else 1 - bit[d1]
        b2 = bit[d2] if not f2 else 1 - bit[d2]
        return bit[d0], b1, b2

    def plane_dev(p, k):
        return dev(PLANE[k][0] * ORDERS[p][1] + PLANE[k][1] * ORDERS[p][2])

    def own_shard(out, p):
        return out.at[out_slot(core, p, *bits(p), 1), :]

    def plane_shard(out, p, k):
        return out.at[out_slot(core, p, *bits(p, *PLANE[k]), 1), :]

    def axis_half(out, p, far):
        b0 = bits(p)[0]
        return out.at[out_slot(core, p, 1 - b0 if far else b0, 0, 0, 4), :]

    def pair_start(t, g, pp):
        send(lambda: (g.at[half(1 - core), :], pp, s_pair.at[t], m_pair.at[t], partner))

    def pair_finish(t, g, pp, ra):
        arrived(pp, m_pair.at[t])
        pp[...] = pp[...] + g[half(core), :]
        for p in range(3):
            send(lambda p=p: (pp.at[slot(p, 1 - bits(p)[0], 0, 0, 4), :],
                              ra.at[pl.ds(SUM_BASE[p] // 2, SUM_ROWS[p] // 2), :],
                              s_r1.at[t, p], m_r1.at[t, p], dev(ORDERS[p][0])))

    def r1_finish(t, pp, ra, rb):
        for p in range(3):
            part = pl.ds(SUM_BASE[p] // 2, SUM_ROWS[p] // 2)
            arrived(ra.at[part, :], m_r1.at[t, p])
            b0, _, _ = bits(p)
            mine = slot(p, b0, 0, 0, 4)
            pp[mine, :] = pp[mine, :] + ra[part, :]
        for k in (2, 0, 1):
            for p in range(3):
                send(lambda p=p, k=k: (pp.at[slot(p, *bits(p, *PLANE[k]), 1), :],
                                       rb.at[k, pl.ds(SUM_BASE[p] // 8, SUM_ROWS[p] // 8), :],
                                       s_r2.at[t, p, k], m_r2.at[t, p, k], plane_dev(p, k)))

    def r2_finish(t, out, pp, rb):
        for p in range(3):
            part = pl.ds(SUM_BASE[p] // 8, SUM_ROWS[p] // 8)
            total = pp[slot(p, *bits(p), 1), :]
            for k in range(3):
                arrived(rb.at[k, part, :], m_r2.at[t, p, k])
                total = total + rb[k, part, :]
            mine = out_slot(core, p, *bits(p), 1)
            out[mine, :] = total
            for k in (2, 0, 1):
                send(lambda p=p, k=k: (own_shard(out, p), own_shard(out, p), s_g1.at[t, p, k], m_g1.at[t, p, k],
                                       plane_dev(p, k)))
            send(lambda p=p: (own_shard(out, p), own_shard(out, p), s_g2.at[t, p, 3], m_g2.at[t, p, 3],
                              dev(ORDERS[p][0])))

    def ag_plane(t, out):
        for k in range(3):
            for p in range(3):
                arrived(plane_shard(out, p, k), m_g1.at[t, p, k])
                send(lambda p=p, k=k: (plane_shard(out, p, k), plane_shard(out, p, k), s_g2.at[t, p, k],
                                       m_g2.at[t, p, k], dev(ORDERS[p][0])))
        for p in range(3):
            send(lambda p=p: (axis_half(out, p, 0), axis_half(out, p, 0), s_fw.at[t, p, 0], m_fw.at[t, p, 0], partner))

    def ag_axis(t, out):
        for p in range(3):
            b0, _, _ = bits(p)
            for k in range(4):
                f1, f2 = PLANE[k] if k < 3 else (0, 0)
                _, b1, b2 = bits(p, f1, f2)
                arrived(out.at[out_slot(core, p, 1 - b0, b1, b2, 1), :], m_g2.at[t, p, k])
            send(lambda p=p: (axis_half(out, p, 1), axis_half(out, p, 1), s_fw.at[t, p, 1], m_fw.at[t, p, 1], partner))

    def ag_finish(t, out):
        for p in range(3):
            b0, _, _ = bits(p)
            arrived(out.at[out_slot(1 - core, p, b0, 0, 0, 4), :], m_fw.at[t, p, 0])
            arrived(out.at[out_slot(1 - core, p, 1 - b0, 0, 0, 4), :], m_fw.at[t, p, 1])

    tower_backward(qx, wqo, a_q, h_q, u_q, r_q, gp_q)
    pair_start(0, gp_q, pp_q)
    gather_jobs(uall, u0[6:], s_u, m_u)
    pair_send(uall, L0, s_ud, m_ud)
    gather_jobs(uall, u1[:3], s_u, m_u)
    pair_finish(0, gp_q, pp_q, ra_q)

    for k in range(NDEV - 1):
        src = (me + NDEV - 1 - k) % NDEV
        arrived(msgs.at[src], m_msg.at[k])
    total = msgs[0, :, ROWS:MSG]
    for b in range(1, NDEV):
        total = total + msgs[b, :, ROWS:MSG]
    loss_out[...] = jnp.broadcast_to(jnp.sum(total, axis=1, keepdims=True) * (1.0 / TOTAL), (1, 128))

    def dv_block(b, own=False):
        s = dot_nt(vall[me], uall[b])
        p = jnp.exp2(s * LOGIT_SCALE - wide(bcol[...])) * msgs[b, :, 0:ROWS]
        if own:
            p = jnp.where(eye, p - 1.0, p)
        return dot_nn(p.astype(BF16), uall[b])

    def dv_group(blocks):
        total = dacc[...]
        for b in blocks:
            total = total + dv_block(b)
        dacc[...] = total

    def dv_step(g, _):
        @pl.when(g == 1)
        def _():
            gather_jobs(uall, u1[3:], s_u, m_u)
            pair_send(uall, L1, s_ud, m_ud)
            pair_wait(uall, L0, m_ud)

        @pl.when(g == 3)
        def _():
            gather_jobs(uall, u2, s_u, m_u)
            pair_send(uall, L2, s_ud, m_ud)
            pair_wait(uall, L1, m_ud)

        dv_group(group_devs(g))
        return 0

    pair_wait(uall, (0,), m_ud)
    dacc[...] = dv_block(me, True) + dv_block(partner)
    lax.fori_loop(0, 4, dv_step, 0)
    r1_finish(0, pp_q, ra_q, rb_q)
    pair_wait(uall, L2, m_ud)
    dv_group([dev(7), dev_other(7)])
    tower_backward(vx, wvo, a_v, h_v, u_v, r_v, gp_v)
    pair_start(1, gp_v, pp_v)
    r2_finish(0, gq_out, pp_q, rb_q)
    pair_finish(1, gp_v, pp_v, ra_v)
    ag_plane(0, gq_out)
    r1_finish(1, pp_v, ra_v, rb_v)
    ag_axis(0, gq_out)
    r2_finish(1, gv_out, pp_v, rb_v)
    ag_finish(0, gq_out)
    ag_plane(1, gv_out)
    ag_axis(1, gv_out)
    ag_finish(1, gv_out)
    for make in pending:
        rcopy(*make()).wait_send()


def finish(loss, gq, gv, loss_out, gqi, gqo, gvi, gvo, sem):
    copies = []
    for i, (g, gi, go) in enumerate(((gq, gqi, gqo), (gv, gvi, gvo))):
        copies.append(pltpu.make_async_copy(g.at[0:FEAT, :], gi.at[:, 0:EMB], sem.at[i, 0]))
        copies.append(pltpu.make_async_copy(g.at[FEAT:2 * FEAT, :], gi.at[:, EMB:HID], sem.at[i, 1]))
        copies.append(pltpu.make_async_copy(g.at[2 * FEAT:PACK, :], go, sem.at[i, 2]))
    for copy in copies:
        copy.start()
    loss_out[0] = loss[0, 0]
    for copy in copies:
        copy.wait()


def solution(mesh):
    vmem = pl.BlockSpec(memory_space=pltpu.VMEM)
    smem = pl.BlockSpec(memory_space=pltpu.SMEM)
    hbm = pl.BlockSpec(memory_space=pltpu.HBM)
    anym = pl.BlockSpec(memory_space=pl.ANY)
    dma = pltpu.SemaphoreType.DMA
    V = pltpu.VMEM

    def local_step(query_feat, item_feat, log_q, w_query_in, w_query_out, w_item_in, w_item_out):
        shape = jax.ShapeDtypeStruct
        loss, gq, gv = pl.pallas_call(
            kernel,
            out_shape=(shape((1, 128), F32), shape((PACK, EMB), F32), shape((PACK, EMB), F32)),
            in_specs=[hbm] * 7,
            out_specs=(vmem, vmem, vmem),
            scratch_shapes=[
                V((ROWS, FEAT), BF16), V((ROWS, FEAT), BF16),
                V((FEAT, HID), BF16), V((HID, EMB), BF16), V((FEAT, HID), BF16), V((HID, EMB), BF16), dma((7,)),
                V((NDEV, ROWS, EMB), BF16), V((NDEV, ROWS, EMB), BF16),
                V((NDEV, 1, ROWS), F32), V((1, 128), F32),
                V((NDEV, 1, MSG), F32),
                V((ROWS, EMB), F32), V((ROWS, EMB), F32),
                V((ROWS, HID), F32), V((ROWS, HID), F32),
                V((ROWS, HID), BF16), V((ROWS, HID), BF16),
                V((ROWS, EMB), F32), V((ROWS, EMB), F32),
                V((ROWS, EMB), F32), V((ROWS, EMB), F32),
                V((ROWS, EMB), F32), V((ROWS, EMB), F32), V((ROWS, EMB), F32),
                V((PACK, EMB), F32), V((PACK, EMB), F32),
                V((HALF, EMB), F32), V((HALF, EMB), F32),
                V((HALF // 2, EMB), F32), V((HALF // 2, EMB), F32),
                V((3, HALF // 8, EMB), F32), V((3, HALF // 8, EMB), F32),
                dma((15,)), dma((15,)),
                dma((4, 8, 3)), dma((4, 8)), dma((8,)), dma((8,)), dma((8,)), dma((8,)),
                dma((3, 8, 3)), dma((3, 8)), dma((8,)), dma((8,)),
                dma((2,)), dma((2,)), dma((2, 3)), dma((2, 3)), dma((2, 3, 3)), dma((2, 3, 3)),
                dma((2, 3, 3)), dma((2, 3, 3)), dma((2, 3, 4)), dma((2, 3, 4)), dma((2, 3, 2)), dma((2, 3, 2)),
            ],
            compiler_params=pltpu.CompilerParams(collective_id=0, has_side_effects=True,
                                                 vmem_limit_bytes=48 * 1024 * 1024),
            name="step",
        )(*(pltpu.with_memory_space_constraint(x, pltpu.HBM) for x in (
            query_feat, item_feat, log_q.reshape(1, ROWS), w_query_in, w_query_out, w_item_in, w_item_out)))
        return pl.pallas_call(
            finish,
            out_shape=(shape((1,), F32), shape((FEAT, HID), F32), shape((HID, EMB), F32),
                       shape((FEAT, HID), F32), shape((HID, EMB), F32)),
            in_specs=[vmem, vmem, vmem],
            out_specs=(smem, hbm, hbm, hbm, hbm),
            scratch_shapes=[dma((2, 3))],
            compiler_params=pltpu.CompilerParams(vmem_limit_bytes=8 * 1024 * 1024),
            name="finish",
        )(loss, gq, gv)

    return jax.shard_map(local_step, mesh=mesh, in_specs=(P('dp', None), P('dp', None), P('dp'), P(), P(), P(), P()), out_specs=(P(), P(), P(), P(), P()), check_vma=False)
```

time: 55.7 us -> 52.5 us (0.943)
  Pallas kernels: 54.9 us -> 51.7 us
    pallas_call x1, Pallas kernels: 53.3 us -> 50.1 us  [local_step(): pl.pallas_call(kernel, out_shape=(shape((1, 128), F32), shape((PACK, EMB)...]
where the time goes in v3:
time: 52.5 us; the launch traced here: 52.3 us
  Pallas kernels  51.7 us (98%)
  between operations  0.64 us (1%)
    pallas_call x1, Pallas kernels, local_step(): pl.pallas_call(kernel, out_shape=(shape((1, 128), F32), shape((PACK, EMB)...  50.1 us
    pallas_call x1, Pallas kernels, local_step(): pl.pallas_call(finish, out_shape=(shape((1,), F32), shape((FEAT, HID), F3...  1.62 us

profile of v3, /device:TPU:0, one launch (start us, length us, event | category | flops | bytes accessed | tf_op | source)
XLA Modules:
  0.0 52.3 jit_solution(16060864635781846417)
XLA Ops:
  0.6 50.1 %step.1 = (f32[1,128]{1,0:T(1,128)S(1)}, f32[1280,128]{1,0:T(8,128)S(1)}, f32[1280,128]{1,0:T(8,128)S(1)}) custom-call(bf16[512,512]{1,0:T(8,128)(2,1)} %qx_h.1, bf16[512,512]{1,0:T(8,128)(2,1)} %vx_h.1, f32[1,512]{1,0:T(1,128)} %bitcast.1, bf16[512,256]{1,0:T(8,128)(2,1)} %wqi_h.1, bf16[256,128]{1,0:T(8,128)(2,1)} %wqo_h.1, bf16[512,256]{1,0:T(8,128)(2,1)} %wvi_h.1, ...), custom_call_target="tpu_custom_call" | custom-call | tf_op jit(solution)/shard_map/step/pallas_call | solution.py:457
  50.7 1.6 %finish.1 = (f32[1]{0:T(128)}, f32[512,256]{1,0:T(8,128)}, f32[256,128]{1,0:T(8,128)}, f32[512,256]{1,0:T(8,128)}, f32[256,128]{1,0:T(8,128)}) custom-call(f32[1,128]{1,0:T(1,128)S(1)} %get-tuple-element.8.loss, f32[1280,128]{1,0:T(8,128)S(1)} %get-tuple-element.9.gq, f32[1280,128]{1,0:T(8,128)S(1)} %get-tuple-element.10.gv), custom_call_target="tpu_custom_call" | custom-call | tf_op jit(solution)/shard_map/finish/pallas_call | solution.py:489

commit v4 on v3

--- a/solution.py
+++ b/solution.py
@@ -24,6 +24,7 @@
 PARTS = ((0, 176), (176, 176), (352, 160))
 ORDERS = ((1, 2, 4), (2, 4, 1), (4, 1, 2), (1, 2, 4))
 LEVELS = ((1, 2, 4), (6, 5, 3), (7,))
+PAIR = ((0,),) + LEVELS
 MSG = ROWS + 128
 F32 = jnp.float32
 BF16 = jnp.bfloat16
@@ -48,11 +49,11 @@
 def kernel(qx_h, vx_h, lq_h, wqi_h, wqo_h, wvi_h, wvo_h,
            loss_out, gq_out, gv_out,
            qx, vx, wqi, wqo, wvi, wvo, s_in,
-           uall, vall, lqall, crun, msgs, lacc, diag,
+           uall, vall, lqall, crun, pos_row, msgs, lacc, diag,
            a_q, a_v, h_q, h_v, u_q, u_v, r_q, r_v, invl, bcol, dacc,
-           gp_q, gp_v, pp_q, pp_v, ra_q, ra_v, rb_q, rb_v,
+           gp_q, gp_v, pp_q, pp_v, ra_q, ra_v, rb_q, rb_v, fin, s_own,
            s_msg, m_msg,
-           s_v, m_v, s_vd, m_vd, s_ld, m_ld, s_u, m_u, s_ud, m_ud,
+           s_v, m_v, m_vd, m_ld, s_u, m_u, m_ud,
            s_pair, m_pair, s_r1, m_r1, s_r2, m_r2, s_g1, m_g1, s_g2, m_g2, s_fw, m_fw):
     me = lax.axis_index("dp")
     core = me % 2
@@ -61,21 +62,33 @@
     partner = me + 1 - 2 * core
     chip = me // 2
 
+    def flipped(mask):
+        return me + (mask % 2) * step_x + ((mask // 2) % 2) * step_y + (mask // 4) * step_z
+
+    same_core = [flipped(mask) for mask in range(8)]
+
     def dev(mask):
-        return me + (mask % 2) * step_x + ((mask // 2) % 2) * step_y + (mask // 4) * step_z
+        return same_core[mask]
 
     def dev_other(mask):
-        return partner + (mask % 2) * step_x + ((mask // 2) % 2) * step_y + (mask // 4) * step_z
+        return same_core[mask] + partner - me
+
+    def nth_dev(n):
+        q, r = (n + 2) // 3, (n + 2) % 3
+        base = r * (r + 1) // 2 + 1
+        last = q // 5
+        mask = (base + q // 3 * (7 - 2 * base)) * ((q + 4) // 5) * (1 - last) + 7 * last
+        return flipped(mask) + ((q + 1) % 2 + last * (n - 13)) * (partner - me)
 
     def rcopy(src, dst, ssem, rsem, to):
         return pltpu.make_async_remote_copy(src_ref=src, dst_ref=dst, send_sem=ssem, recv_sem=rsem,
                                             device_id=(to,), device_id_type=MESH)
 
-    pending = []
-
-    def send(make):
-        rcopy(*make()).start()
-        pending.append(make)
+    def send(src, dst, ssem, rsem, to):
+        rcopy(src, dst, ssem, rsem, to).start()
+
+    def sent(like, ssem):
+        rcopy(like, like, ssem, ssem, partner).wait_send()
 
     def arrived(ref, rsem):
         rcopy(ref, ref, rsem, rsem, partner).wait_recv()
@@ -114,7 +127,8 @@
 
     def send_part(ref, p, m, t, ss, ms):
         d = ORDERS[p][t]
-        send(lambda: (part_ref(ref, dev(m), p), part_ref(ref, dev(m), p), ss.at[p, m, t], ms.at[p, m + d], dev(d)))
+        src = part_ref(ref, dev(m), p)
+        send(src, src, ss.at[p // 3], ms.at[p % 3, m + d], dev(d))
 
     def gather_own(ref, ts, ps, ss, ms):
         for t in ts:
@@ -132,27 +146,31 @@
     def gather_jobs(ref, jobs, ss, ms):
         for top, p, m in jobs:
             src = dev(m)
-            arrived(part_ref(ref, src, p), ms.at[p, m])
+            if p == 0 and ref is vall:
+                arrived(ref.at[src, 0:PARTS[0][1] + 8, :], ms.at[0, m])
+                for t in range(top + 1, 3):
+                    send_part(ref, 3, m, t, ss, ms)
+            else:
+                arrived(part_ref(ref, src, p), ms.at[p, m])
             for t in range(top + 1, 3):
                 send_part(ref, p, m, t, ss, ms)
 
-    def pair_send(ref, masks, sd, md):
-        for m in masks:
-            send(lambda m=m: (ref.at[dev(m)], ref.at[dev(m)], sd.at[m], md.at[m], partner))
-
-    def pair_wait(ref, masks, md):
-        for m in masks:
-            arrived(ref.at[dev_other(m)], md.at[m])
+    def pair_send(ref, level, sd, md):
+        for m in PAIR[level]:
+            send(ref.at[dev(m)], ref.at[dev(m)], sd, md.at[level], partner)
+
+    def pair_wait(ref, level, md):
+        arrived(ref.at[0:len(PAIR[level])], md.at[level])
 
     VP, UP = (3, 0, 1, 2), (0, 1, 2)
-    pair_send(lqall, (0,), s_ld, m_ld)
-    pair_send(vall, (0,), s_vd, m_vd)
+    pair_send(lqall, 0, s_v.at[3], m_ld)
+    pair_send(vall, 0, s_v.at[2], m_vd)
     gather_own(vall, (0, 1, 2), VP, s_v, m_v)
 
     for load in loads[4:]:
         load.wait()
     tower_forward(qx, wqi, wqo, a_q, h_q, u_q, r_q, uall)
-    pair_send(uall, (0,), s_ud, m_ud)
+    pair_send(uall, 0, s_u.at[1], m_ud)
 
     eye = (lax.broadcasted_iota(jnp.int32, (ROWS, ROWS), 0)
            == lax.broadcasted_iota(jnp.int32, (ROWS, ROWS), 1))
@@ -187,67 +205,62 @@
     lacc[...] = lane_sum(e_own)
     diag[...] = jnp.broadcast_to(jnp.sum(jnp.where(eye, e_own, 0.0), axis=1, keepdims=True), (ROWS, EMB))
     dacc[...] = dot_nn(jnp.where(eye, 0.0, e_own).astype(BF16), vall[me])
-    pair_wait(lqall, (0,), m_ld)
-    pair_wait(vall, (0,), m_vd)
-    exp_group((partner,))
-
-    L0, L1, L2 = LEVELS
-    v0, v1, v2 = (level_jobs(k, VP) for k in range(3))
+    pos_row[...] = jnp.sum((uall[me].astype(F32) * vall[me].astype(F32)).T, axis=0, keepdims=True) * (1.0 / TEMPERATURE)
+
+    v0, v1, v2 = (level_jobs(k, UP) for k in range(3))
     u0, u1, u2 = (level_jobs(k, UP) for k in range(3))
-
-    def group_devs(g):
-        masks = [b + (g // 2) * (7 - 2 * b) for b in L0]
-        return [dev(m) + (g % 2) * (partner - me) for m in masks]
 
     def exp_step(g, _):
         @pl.when(g == 0)
         def _():
             gather_jobs(vall, v0, s_v, m_v)
-            pair_send(lqall, L0, s_ld, m_ld)
-            pair_send(vall, L0, s_vd, m_vd)
+            pair_send(lqall, 1, s_v.at[3], m_ld)
+            pair_send(vall, 1, s_v.at[2], m_vd)
+            pair_wait(lqall, 0, m_ld)
+            pair_wait(vall, 0, m_vd)
 
         @pl.when(g == 1)
         def _():
-            gather_jobs(vall, v1[:4], s_v, m_v)
+            gather_jobs(vall, v1[:3], s_v, m_v)
             gather_own(uall, (0, 1, 2), UP, s_u, m_u)
-            pair_wait(lqall, L0, m_ld)
-            pair_wait(vall, L0, m_vd)
+            pair_wait(lqall, 1, m_ld)
+            pair_wait(vall, 1, m_vd)
 
         @pl.when(g == 2)
         def _():
-            gather_jobs(vall, v1[4:], s_v, m_v)
-            pair_send(lqall, L1, s_ld, m_ld)
-            pair_send(vall, L1, s_vd, m_vd)
+            gather_jobs(vall, v1[3:], s_v, m_v)
+            pair_send(lqall, 2, s_v.at[3], m_ld)
+            pair_send(vall, 2, s_v.at[2], m_vd)
 
         @pl.when(g == 3)
         def _():
             gather_jobs(vall, v2, s_v, m_v)
-            pair_send(lqall, L2, s_ld, m_ld)
-            pair_send(vall, L2, s_vd, m_vd)
-            pair_wait(lqall, L1, m_ld)
-            pair_wait(vall, L1, m_vd)
-
-        exp_group(group_devs(g))
+            pair_send(lqall, 3, s_v.at[3], m_ld)
+            pair_send(vall, 3, s_v.at[2], m_vd)
+            pair_wait(lqall, 2, m_ld)
+            pair_wait(vall, 2, m_vd)
+
+        @pl.when(g == 4)
+        def _():
+            gather_jobs(uall, u0[:3], s_u, m_u)
+            pair_wait(lqall, 3, m_ld)
+            pair_wait(vall, 3, m_vd)
+
+        exp_group([nth_dev(3 * g + j) for j in range(3)])
         return 0
 
-    lax.fori_loop(0, 4, exp_step, 0)
-    gather_jobs(uall, u0[:3], s_u, m_u)
-    pair_wait(lqall, L2, m_ld)
-    pair_wait(vall, L2, m_vd)
-    exp_group((dev(7), dev_other(7)))
+    lax.fori_loop(0, 5, exp_step, 0)
 
     acc = lacc[...]
     shift = crun[0:1, 0:1]
     lq_own = lqall[me]
     l_row = jnp.sum(acc.T, axis=0, keepdims=True)
-    pos = (uall[me].astype(F32) * vall[me].astype(F32)).T
-    pos_row = jnp.sum(pos, axis=0, keepdims=True)
-    loss_row = jnp.log(l_row) + ((shift + lq_own) - pos_row * (1.0 / TEMPERATURE))
+    loss_row = jnp.log(l_row) + ((shift + lq_own) - pos_row[...])
     loss_part = loss_row[:, 0:128] + loss_row[:, 128:256] + (loss_row[:, 256:384] + loss_row[:, 384:512])
     msgs[me, :, 0:ROWS] = 1.0 / l_row
     msgs[me, :, ROWS:MSG] = loss_part
     for k in range(NDEV - 1):
-        send(lambda k=k: (msgs.at[me], msgs.at[me], s_msg.at[k], m_msg.at[k], others[k]))
+        send(msgs.at[me], msgs.at[me], s_msg.at[0], m_msg.at[0], others[k])
     invl[...] = jnp.broadcast_to(1.0 / jnp.sum(acc, axis=1, keepdims=True), (ROWS, EMB))
     bcol[...] = jnp.broadcast_to((lq_own + shift) * LOG2E, (EMB, ROWS)).T
 
@@ -292,8 +305,8 @@
     def plane_dev(p, k):
         return dev(PLANE[k][0] * ORDERS[p][1] + PLANE[k][1] * ORDERS[p][2])
 
-    def own_shard(out, p):
-        return out.at[out_slot(core, p, *bits(p), 1), :]
+    def like_shard(out, p):
+        return out.at[0:SUM_ROWS[p] // 8, :]
 
     def plane_shard(out, p, k):
         return out.at[out_slot(core, p, *bits(p, *PLANE[k]), 1), :]
@@ -303,15 +316,14 @@
         return out.at[out_slot(core, p, 1 - b0 if far else b0, 0, 0, 4), :]
 
     def pair_start(t, g, pp):
-        send(lambda: (g.at[half(1 - core), :], pp, s_pair.at[t], m_pair.at[t], partner))
+        send(g.at[half(1 - core), :], pp, s_pair.at[t], m_pair.at[t], partner)
 
     def pair_finish(t, g, pp, ra):
         arrived(pp, m_pair.at[t])
         pp[...] = pp[...] + g[half(core), :]
         for p in range(3):
-            send(lambda p=p: (pp.at[slot(p, 1 - bits(p)[0], 0, 0, 4), :],
-                              ra.at[pl.ds(SUM_BASE[p] // 2, SUM_ROWS[p] // 2), :],
-                              s_r1.at[t, p], m_r1.at[t, p], dev(ORDERS[p][0])))
+            part = ra.at[pl.ds(SUM_BASE[p] // 2, SUM_ROWS[p] // 2), :]
+            send(pp.at[slot(p, 1 - bits(p)[0], 0, 0, 4), :], part, s_r1.at[t], m_r1.at[t, p], dev(ORDERS[p][0]))
 
     def r1_finish(t, pp, ra, rb):
         for p in range(3):
@@ -322,59 +334,61 @@
             pp[mine, :] = pp[mine, :] + ra[part, :]
         for k in (2, 0, 1):
             for p in range(3):
-                send(lambda p=p, k=k: (pp.at[slot(p, *bits(p, *PLANE[k]), 1), :],
-                                       rb.at[k, pl.ds(SUM_BASE[p] // 8, SUM_ROWS[p] // 8), :],
-                                       s_r2.at[t, p, k], m_r2.at[t, p, k], plane_dev(p, k)))
+                part = rb.at[k, pl.ds(SUM_BASE[p] // 8, SUM_ROWS[p] // 8), :]
+                send(pp.at[slot(p, *bits(p, *PLANE[k]), 1), :], part, s_r2.at[t], m_r2.at[t, p], plane_dev(p, k))
 
     def r2_finish(t, out, pp, rb):
         for p in range(3):
             part = pl.ds(SUM_BASE[p] // 8, SUM_ROWS[p] // 8)
             total = pp[slot(p, *bits(p), 1), :]
+            arrived(rb.at[:, part, :], m_r2.at[t, p])
             for k in range(3):
-                arrived(rb.at[k, part, :], m_r2.at[t, p, k])
                 total = total + rb[k, part, :]
-            mine = out_slot(core, p, *bits(p), 1)
-            out[mine, :] = total
+            own = fin.at[t, pl.ds(SUM_BASE[p] // 8, SUM_ROWS[p] // 8), :]
+            fin[t, SUM_BASE[p] // 8:(SUM_BASE[p] + SUM_ROWS[p]) // 8, :] = total
+            place = out.at[out_slot(core, p, *bits(p), 1), :]
+            keep = pltpu.make_async_copy(own, place, s_own.at[t, p])
+            keep.start()
             for k in (2, 0, 1):
-                send(lambda p=p, k=k: (own_shard(out, p), own_shard(out, p), s_g1.at[t, p, k], m_g1.at[t, p, k],
-                                       plane_dev(p, k)))
-            send(lambda p=p: (own_shard(out, p), own_shard(out, p), s_g2.at[t, p, 3], m_g2.at[t, p, 3],
-                              dev(ORDERS[p][0])))
+                send(own, place, s_g1.at[t], m_g1.at[t, p, k], plane_dev(p, k))
+            send(own, place, s_g2.at[t], m_g2.at[t, p], dev(ORDERS[p][0]))
 
     def ag_plane(t, out):
         for k in range(3):
             for p in range(3):
-                arrived(plane_shard(out, p, k), m_g1.at[t, p, k])
-                send(lambda p=p, k=k: (plane_shard(out, p, k), plane_shard(out, p, k), s_g2.at[t, p, k],
-                                       m_g2.at[t, p, k], dev(ORDERS[p][0])))
+                ref = plane_shard(out, p, k)
+                arrived(ref, m_g1.at[t, p, k])
+                send(ref, ref, s_g2.at[t], m_g2.at[t, p], dev(ORDERS[p][0]))
         for p in range(3):
-            send(lambda p=p: (axis_half(out, p, 0), axis_half(out, p, 0), s_fw.at[t, p, 0], m_fw.at[t, p, 0], partner))
+            pltpu.make_async_copy(like_shard(out, p), like_shard(out, p), s_own.at[t, p]).wait()
+            ref = axis_half(out, p, 0)
+            send(ref, ref, s_fw.at[t], m_fw.at[t], partner)
 
     def ag_axis(t, out):
         for p in range(3):
-            b0, _, _ = bits(p)
-            for k in range(4):
-                f1, f2 = PLANE[k] if k < 3 else (0, 0)
-                _, b1, b2 = bits(p, f1, f2)
-                arrived(out.at[out_slot(core, p, 1 - b0, b1, b2, 1), :], m_g2.at[t, p, k])
-            send(lambda p=p: (axis_half(out, p, 1), axis_half(out, p, 1), s_fw.at[t, p, 1], m_fw.at[t, p, 1], partner))
+            ref = axis_half(out, p, 1)
+            arrived(ref, m_g2.at[t, p])
+            send(ref, ref, s_fw.at[t], m_fw.at[t], partner)
 
     def ag_finish(t, out):
-        for p in range(3):
-            b0, _, _ = bits(p)
-            arrived(out.at[out_slot(1 - core, p, b0, 0, 0, 4), :], m_fw.at[t, p, 0])
-            arrived(out.at[out_slot(1 - core, p, 1 - b0, 0, 0, 4), :], m_fw.at[t, p, 1])
+        arrived(out.at[0:HALF, :], m_fw.at[t])
+
+    def sums_sent(t, out, pp, ra, rb):
+        sent(pp, s_pair.at[t])
+        sent(ra, s_r1.at[t])
+        sent(rb, s_r2.at[t])
+        sent(rb, s_g1.at[t])
+        sent(ra, s_g2.at[t])
+        sent(pp, s_fw.at[t])
 
     tower_backward(qx, wqo, a_q, h_q, u_q, r_q, gp_q)
     pair_start(0, gp_q, pp_q)
     gather_jobs(uall, u0[6:], s_u, m_u)
-    pair_send(uall, L0, s_ud, m_ud)
+    pair_send(uall, 1, s_u.at[1], m_ud)
     gather_jobs(uall, u1[:3], s_u, m_u)
     pair_finish(0, gp_q, pp_q, ra_q)
 
-    for k in range(NDEV - 1):
-        src = (me + NDEV - 1 - k) % NDEV
-        arrived(msgs.at[src], m_msg.at[k])
+    arrived(msgs.at[0:NDEV - 1], m_msg.at[0])
     total = msgs[0, :, ROWS:MSG]
     for b in range(1, NDEV):
         total = total + msgs[b, :, ROWS:MSG]
@@ -397,38 +411,50 @@
         @pl.when(g == 1)
         def _():
             gather_jobs(uall, u1[3:], s_u, m_u)
-            pair_send(uall, L1, s_ud, m_ud)
-            pair_wait(uall, L0, m_ud)
+            pair_send(uall, 2, s_u.at[1], m_ud)
+            pair_wait(uall, 1, m_ud)
+
+        @pl.when(g == 2)
+        def _():
+            r1_finish(0, pp_q, ra_q, rb_q)
 
         @pl.when(g == 3)
         def _():
             gather_jobs(uall, u2, s_u, m_u)
-            pair_send(uall, L2, s_ud, m_ud)
-            pair_wait(uall, L1, m_ud)
-
-        dv_group(group_devs(g))
+            pair_send(uall, 3, s_u.at[1], m_ud)
+            pair_wait(uall, 2, m_ud)
+
+        @pl.when(g == 4)
+        def _():
+            pair_wait(uall, 3, m_ud)
+            r2_finish(0, gq_out, pp_q, rb_q)
+
+        dv_group([nth_dev(3 * g + j) for j in range(3)])
         return 0
 
-    pair_wait(uall, (0,), m_ud)
-    dacc[...] = dv_block(me, True) + dv_block(partner)
-    lax.fori_loop(0, 4, dv_step, 0)
-    r1_finish(0, pp_q, ra_q, rb_q)
-    pair_wait(uall, L2, m_ud)
-    dv_group([dev(7), dev_other(7)])
+    pair_wait(uall, 0, m_ud)
+    dacc[...] = dv_block(me, True)
+    lax.fori_loop(0, 5, dv_step, 0)
     tower_backward(vx, wvo, a_v, h_v, u_v, r_v, gp_v)
     pair_start(1, gp_v, pp_v)
-    r2_finish(0, gq_out, pp_q, rb_q)
+    sent(vall.at[0:7], s_v.at[0])
+    sent(lqall.at[0:7], s_v.at[1])
+    sent(vall.at[0:8], s_v.at[2])
+    sent(lqall.at[0:8], s_v.at[3])
+    sent(uall.at[0:7], s_u.at[0])
+    sent(uall.at[0:8], s_u.at[1])
+    sent(msgs.at[0:NDEV - 1], s_msg.at[0])
     pair_finish(1, gp_v, pp_v, ra_v)
     ag_plane(0, gq_out)
     r1_finish(1, pp_v, ra_v, rb_v)
     ag_axis(0, gq_out)
     r2_finish(1, gv_out, pp_v, rb_v)
     ag_finish(0, gq_out)
+    sums_sent(0, gq_out, pp_q, ra_q, rb_q)
     ag_plane(1, gv_out)
     ag_axis(1, gv_out)
     ag_finish(1, gv_out)
-    for make in pending:
-        rcopy(*make()).wait_send()
+    sums_sent(1, gv_out, pp_v, ra_v, rb_v)
 
 
 def finish(loss, gq, gv, loss_out, gqi, gqo, gvi, gvo, sem):
@@ -458,12 +484,12 @@
             kernel,
             out_shape=(shape((1, 128), F32), shape((PACK, EMB), F32), shape((PACK, EMB), F32)),
             in_specs=[hbm] * 7,
-            out_specs=(vmem, vmem, vmem),
+            out_specs=(vmem, anym, anym),
             scratch_shapes=[
                 V((ROWS, FEAT), BF16), V((ROWS, FEAT), BF16),
                 V((FEAT, HID), BF16), V((HID, EMB), BF16), V((FEAT, HID), BF16), V((HID, EMB), BF16), dma((7,)),
                 V((NDEV, ROWS, EMB), BF16), V((NDEV, ROWS, EMB), BF16),
-                V((NDEV, 1, ROWS), F32), V((1, 128), F32),
+                V((NDEV, 1, ROWS), F32), V((1, 128), F32), V((1, ROWS), F32),
                 V((NDEV, 1, MSG), F32),
                 V((ROWS, EMB), F32), V((ROWS, EMB), F32),
                 V((ROWS, HID), F32), V((ROWS, HID), F32),
@@ -474,12 +500,11 @@
                 V((PACK, EMB), F32), V((PACK, EMB), F32),
                 V((HALF, EMB), F32), V((HALF, EMB), F32),
                 V((HALF // 2, EMB), F32), V((HALF // 2, EMB), F32),
-                V((3, HALF // 8, EMB), F32), V((3, HALF // 8, EMB), F32),
-                dma((15,)), dma((15,)),
-                dma((4, 8, 3)), dma((4, 8)), dma((8,)), dma((8,)), dma((8,)), dma((8,)),
-                dma((3, 8, 3)), dma((3, 8)), dma((8,)), dma((8,)),
-                dma((2,)), dma((2,)), dma((2, 3)), dma((2, 3)), dma((2, 3, 3)), dma((2, 3, 3)),
-                dma((2, 3, 3)), dma((2, 3, 3)), dma((2, 3, 4)), dma((2, 3, 4)), dma((2, 3, 2)), dma((2, 3, 2)),
+                V((3, HALF // 8, EMB), F32), V((3, HALF // 8, EMB), F32), V((2, HALF // 8, EMB), F32), dma((2, 3)),
+                dma((1,)), dma((1,)),
+                dma((4,)), dma((3, 8)), dma((4,)), dma((4,)), dma((2,)), dma((3, 8)), dma((4,)),
+                dma((2,)), dma((2,)), dma((2,)), dma((2, 3)), dma((2,)), dma((2, 3)),
+                dma((2,)), dma((2, 3, 3)), dma((2,)), dma((2, 3)), dma((2,)), dma((2,)),
             ],
             compiler_params=pltpu.CompilerParams(collective_id=0, has_side_effects=True,
                                                  vmem_limit_bytes=48 * 1024 * 1024),
@@ -490,7 +515,7 @@
             finish,
             out_shape=(shape((1,), F32), shape((FEAT, HID), F32), shape((HID, EMB), F32),
                        shape((FEAT, HID), F32), shape((HID, EMB), F32)),
-            in_specs=[vmem, vmem, vmem],
+            in_specs=[vmem, anym, anym],
             out_specs=(smem, hbm, hbm, hbm, hbm),
             scratch_shapes=[dma((2, 3))],
             compiler_params=pltpu.CompilerParams(vmem_limit_bytes=8 * 1024 * 1024),

time: 52.5 us -> 49.1 us (0.935)
  Pallas kernels: 51.7 us -> 48.3 us
    pallas_call x1, Pallas kernels: 50.1 us -> 46.7 us  [local_step(): pl.pallas_call(kernel, out_shape=(shape((1, 128), F32), shape((PACK, EMB)...]
where the time goes in v4:
time: 49.1 us; the launch traced here: 48.9 us
  Pallas kernels  48.3 us (98%)
  between operations  0.64 us (1%)
    pallas_call x1, Pallas kernels, local_step(): pl.pallas_call(kernel, out_shape=(shape((1, 128), F32), shape((PACK, EMB)...  46.7 us
    pallas_call x1, Pallas kernels, local_step(): pl.pallas_call(finish, out_shape=(shape((1,), F32), shape((FEAT, HID), F3...  1.62 us

profile of v4, /device:TPU:0, one launch (start us, length us, event | category | flops | bytes accessed | tf_op | source)
XLA Modules:
  0.0 48.9 jit_solution(2521475764470270490)
XLA Ops:
  0.6 46.7 %step.1 = (f32[1,128]{1,0:T(1,128)S(1)}, f32[1280,128]{1,0:T(8,128)S(1)}, f32[1280,128]{1,0:T(8,128)S(1)}) custom-call(bf16[512,512]{1,0:T(8,128)(2,1)} %qx_h.1, bf16[512,512]{1,0:T(8,128)(2,1)} %vx_h.1, f32[1,512]{1,0:T(1,128)} %bitcast.1, bf16[512,256]{1,0:T(8,128)(2,1)} %wqi_h.1, bf16[256,128]{1,0:T(8,128)(2,1)} %wqo_h.1, bf16[512,256]{1,0:T(8,128)(2,1)} %wvi_h.1, ...), custom_call_target="tpu_custom_call" | custom-call | tf_op jit(solution)/shard_map/step/pallas_call | solution.py:483
  47.3 1.6 %finish.1 = (f32[1]{0:T(128)}, f32[512,256]{1,0:T(8,128)}, f32[256,128]{1,0:T(8,128)}, f32[512,256]{1,0:T(8,128)}, f32[256,128]{1,0:T(8,128)}) custom-call(f32[1,128]{1,0:T(1,128)S(1)} %get-tuple-element.8.loss, f32[1280,128]{1,0:T(8,128)S(1)} %get-tuple-element.9.gq, f32[1280,128]{1,0:T(8,128)S(1)} %get-tuple-element.10.gv), custom_call_target="tpu_custom_call" | custom-call | tf_op jit(solution)/shard_map/finish/pallas_call | solution.py:514

commit v5 on v4

--- a/solution.py
+++ b/solution.py
@@ -25,6 +25,7 @@
 ORDERS = ((1, 2, 4), (2, 4, 1), (4, 1, 2), (1, 2, 4))
 LEVELS = ((1, 2, 4), (6, 5, 3), (7,))
 PAIR = ((0,),) + LEVELS
+SLOT = {(0, 0): 0, (0, 1): 1, (0, 2): 2, (1, 1): 3, (1, 2): 4, (2, 2): 5}
 MSG = ROWS + 128
 F32 = jnp.float32
 BF16 = jnp.bfloat16
@@ -53,7 +54,7 @@
            a_q, a_v, h_q, h_v, u_q, u_v, r_q, r_v, invl, bcol, dacc,
            gp_q, gp_v, pp_q, pp_v, ra_q, ra_v, rb_q, rb_v, fin, s_own,
            s_msg, m_msg,
-           s_v, m_v, m_vd, m_ld, s_u, m_u, m_ud,
+           s_v, m_v, m_l, m_vd, m_ld, s_u, m_u, m_ud,
            s_pair, m_pair, s_r1, m_r1, s_r2, m_r2, s_g1, m_g1, s_g2, m_g2, s_fw, m_fw):
     me = lax.axis_index("dp")
     core = me % 2
@@ -128,32 +129,29 @@
     def send_part(ref, p, m, t, ss, ms):
         d = ORDERS[p][t]
         src = part_ref(ref, dev(m), p)
-        send(src, src, ss.at[p // 3], ms.at[p % 3, m + d], dev(d))
-
-    def gather_own(ref, ts, ps, ss, ms):
+        to = m + d
+        rsem = ms.at[to] if p == 3 else ms.at[SLOT[bin(to).count("1") - 1, top_turn(p, to)]]
+        send(src, src, ss.at[p // 3], rsem, dev(d))
+
+    def gather_own(ref, ts, ss, ms):
         for t in ts:
-            for p in ps:
+            for p in range(3):
                 send_part(ref, p, 0, t, ss, ms)
 
-    def level_jobs(level, ps):
-        jobs = []
-        for p in ps:
-            for m in LEVELS[level]:
-                top = max(t for t in range(3) if ORDERS[p][t] & m)
-                jobs.append((top, p, m))
-        return sorted(jobs)
-
-    def gather_jobs(ref, jobs, ss, ms):
-        for top, p, m in jobs:
-            src = dev(m)
-            if p == 0 and ref is vall:
-                arrived(ref.at[src, 0:PARTS[0][1] + 8, :], ms.at[0, m])
-                for t in range(top + 1, 3):
-                    send_part(ref, 3, m, t, ss, ms)
-            else:
-                arrived(part_ref(ref, src, p), ms.at[p, m])
-            for t in range(top + 1, 3):
-                send_part(ref, p, m, t, ss, ms)
+    def top_turn(p, m):
+        return max(t for t in range(3) if ORDERS[p][t] & m)
+
+    def gather_jobs(ref, level, t, ss, ms, ml=None):
+        jobs = [(p, m) for p in range(3) for m in LEVELS[level] if top_turn(p, m) == t]
+        arrived(ref.at[0:len(jobs) // 3] if len(jobs) > 3 else ref.at[0], ms.at[SLOT[level, t]])
+        if ml is not None:
+            for m in sorted({m for m in LEVELS[level] if top_turn(3, m) == t}):
+                arrived(lqall.at[dev(m)], ml.at[m])
+                for tt in range(t + 1, 3):
+                    send_part(lqall, 3, m, tt, ss, ml)
+        for p, m in jobs:
+            for tt in range(t + 1, 3):
+                send_part(ref, p, m, tt, ss, ms)
 
     def pair_send(ref, level, sd, md):
         for m in PAIR[level]:
@@ -162,10 +160,11 @@
     def pair_wait(ref, level, md):
         arrived(ref.at[0:len(PAIR[level])], md.at[level])
 
-    VP, UP = (3, 0, 1, 2), (0, 1, 2)
     pair_send(lqall, 0, s_v.at[3], m_ld)
     pair_send(vall, 0, s_v.at[2], m_vd)
-    gather_own(vall, (0, 1, 2), VP, s_v, m_v)
+    for t in range(3):
+        send_part(lqall, 3, 0, t, s_v, m_l)
+    gather_own(vall, (0, 1, 2), s_v, m_v)
 
     for load in loads[4:]:
         load.wait()
@@ -207,13 +206,11 @@
     dacc[...] = dot_nn(jnp.where(eye, 0.0, e_own).astype(BF16), vall[me])
     pos_row[...] = jnp.sum((uall[me].astype(F32) * vall[me].astype(F32)).T, axis=0, keepdims=True) * (1.0 / TEMPERATURE)
 
-    v0, v1, v2 = (level_jobs(k, UP) for k in range(3))
-    u0, u1, u2 = (level_jobs(k, UP) for k in range(3))
-
     def exp_step(g, _):
         @pl.when(g == 0)
         def _():
-            gather_jobs(vall, v0, s_v, m_v)
+            for t in range(3):
+                gather_jobs(vall, 0, t, s_v, m_v, m_l)
             pair_send(lqall, 1, s_v.at[3], m_ld)
             pair_send(vall, 1, s_v.at[2], m_vd)
             pair_wait(lqall, 0, m_ld)
@@ -221,20 +218,20 @@
 
         @pl.when(g == 1)
         def _():
-            gather_jobs(vall, v1[:3], s_v, m_v)
-            gather_own(uall, (0, 1, 2), UP, s_u, m_u)
+            gather_jobs(vall, 1, 1, s_v, m_v, m_l)
+            gather_own(uall, (0, 1, 2), s_u, m_u)
             pair_wait(lqall, 1, m_ld)
             pair_wait(vall, 1, m_vd)
 
         @pl.when(g == 2)
         def _():
-            gather_jobs(vall, v1[3:], s_v, m_v)
+            gather_jobs(vall, 1, 2, s_v, m_v, m_l)
             pair_send(lqall, 2, s_v.at[3], m_ld)
             pair_send(vall, 2, s_v.at[2], m_vd)
 
         @pl.when(g == 3)
         def _():
-            gather_jobs(vall, v2, s_v, m_v)
+            gather_jobs(vall, 2, 2, s_v, m_v, m_l)
             pair_send(lqall, 3, s_v.at[3], m_ld)
             pair_send(vall, 3, s_v.at[2], m_vd)
             pair_wait(lqall, 2, m_ld)
@@ -242,7 +239,7 @@
 
         @pl.when(g == 4)
         def _():
-            gather_jobs(uall, u0[:3], s_u, m_u)
+            gather_jobs(uall, 0, 0, s_u, m_u)
             pair_wait(lqall, 3, m_ld)
             pair_wait(vall, 3, m_vd)
 
@@ -266,7 +263,7 @@
 
     p_own = diag[...] * jnp.exp2((c_own - crun[...]) * LOG2E) * invl[...]
     dacc[...] = dacc[...] * invl[...] + (p_own - 1.0).astype(BF16).astype(F32) * vall[me].astype(F32)
-    gather_jobs(uall, u0[3:6], s_u, m_u)
+    gather_jobs(uall, 0, 1, s_u, m_u)
 
     def tower_backward(x, w_out, a_ref, h_ref, u_ref, r_ref, g):
         du = dacc[...] * GRAD_SCALE
@@ -305,9 +302,6 @@
     def plane_dev(p, k):
         return dev(PLANE[k][0] * ORDERS[p][1] + PLANE[k][1] * ORDERS[p][2])
 
-    def like_shard(out, p):
-        return out.at[0:SUM_ROWS[p] // 8, :]
-
     def plane_shard(out, p, k):
         return out.at[out_slot(core, p, *bits(p, *PLANE[k]), 1), :]
 
@@ -323,51 +317,51 @@
         pp[...] = pp[...] + g[half(core), :]
         for p in range(3):
             part = ra.at[pl.ds(SUM_BASE[p] // 2, SUM_ROWS[p] // 2), :]
-            send(pp.at[slot(p, 1 - bits(p)[0], 0, 0, 4), :], part, s_r1.at[t], m_r1.at[t, p], dev(ORDERS[p][0]))
+            send(pp.at[slot(p, 1 - bits(p)[0], 0, 0, 4), :], part, s_r1.at[t], m_r1.at[t], dev(ORDERS[p][0]))
 
     def r1_finish(t, pp, ra, rb):
+        arrived(ra, m_r1.at[t])
         for p in range(3):
             part = pl.ds(SUM_BASE[p] // 2, SUM_ROWS[p] // 2)
-            arrived(ra.at[part, :], m_r1.at[t, p])
             b0, _, _ = bits(p)
             mine = slot(p, b0, 0, 0, 4)
             pp[mine, :] = pp[mine, :] + ra[part, :]
         for k in (2, 0, 1):
             for p in range(3):
                 part = rb.at[k, pl.ds(SUM_BASE[p] // 8, SUM_ROWS[p] // 8), :]
-                send(pp.at[slot(p, *bits(p, *PLANE[k]), 1), :], part, s_r2.at[t], m_r2.at[t, p], plane_dev(p, k))
+                send(pp.at[slot(p, *bits(p, *PLANE[k]), 1), :], part, s_r2.at[t], m_r2.at[t], plane_dev(p, k))
 
     def r2_finish(t, out, pp, rb):
+        arrived(rb, m_r2.at[t])
         for p in range(3):
             part = pl.ds(SUM_BASE[p] // 8, SUM_ROWS[p] // 8)
             total = pp[slot(p, *bits(p), 1), :]
-            arrived(rb.at[:, part, :], m_r2.at[t, p])
             for k in range(3):
                 total = total + rb[k, part, :]
             own = fin.at[t, pl.ds(SUM_BASE[p] // 8, SUM_ROWS[p] // 8), :]
             fin[t, SUM_BASE[p] // 8:(SUM_BASE[p] + SUM_ROWS[p]) // 8, :] = total
             place = out.at[out_slot(core, p, *bits(p), 1), :]
-            keep = pltpu.make_async_copy(own, place, s_own.at[t, p])
+            keep = pltpu.make_async_copy(own, place, s_own.at[t])
             keep.start()
             for k in (2, 0, 1):
-                send(own, place, s_g1.at[t], m_g1.at[t, p, k], plane_dev(p, k))
-            send(own, place, s_g2.at[t], m_g2.at[t, p], dev(ORDERS[p][0]))
+                send(own, place, s_g1.at[t], m_g1.at[t, k], plane_dev(p, k))
+            send(own, place, s_g2.at[t], m_g2.at[t], dev(ORDERS[p][0]))
 
     def ag_plane(t, out):
         for k in range(3):
+            arrived(out.at[0:HALF // 8, :], m_g1.at[t, k])
             for p in range(3):
                 ref = plane_shard(out, p, k)
-                arrived(ref, m_g1.at[t, p, k])
-                send(ref, ref, s_g2.at[t], m_g2.at[t, p], dev(ORDERS[p][0]))
+                send(ref, ref, s_g2.at[t], m_g2.at[t], dev(ORDERS[p][0]))
+        pltpu.make_async_copy(fin.at[t], out.at[0:HALF // 8, :], s_own.at[t]).wait()
         for p in range(3):
-            pltpu.make_async_copy(like_shard(out, p), like_shard(out, p), s_own.at[t, p]).wait()
             ref = axis_half(out, p, 0)
             send(ref, ref, s_fw.at[t], m_fw.at[t], partner)
 
     def ag_axis(t, out):
+        arrived(out.at[0:HALF // 2, :], m_g2.at[t])
         for p in range(3):
             ref = axis_half(out, p, 1)
-            arrived(ref, m_g2.at[t, p])
             send(ref, ref, s_fw.at[t], m_fw.at[t], partner)
 
     def ag_finish(t, out):
@@ -381,19 +375,6 @@
         sent(ra, s_g2.at[t])
         sent(pp, s_fw.at[t])
 
-    tower_backward(qx, wqo, a_q, h_q, u_q, r_q, gp_q)
-    pair_start(0, gp_q, pp_q)
-    gather_jobs(uall, u0[6:], s_u, m_u)
-    pair_send(uall, 1, s_u.at[1], m_ud)
-    gather_jobs(uall, u1[:3], s_u, m_u)
-    pair_finish(0, gp_q, pp_q, ra_q)
-
-    arrived(msgs.at[0:NDEV - 1], m_msg.at[0])
-    total = msgs[0, :, ROWS:MSG]
-    for b in range(1, NDEV):
-        total = total + msgs[b, :, ROWS:MSG]
-    loss_out[...] = jnp.broadcast_to(jnp.sum(total, axis=1, keepdims=True) * (1.0 / TOTAL), (1, 128))
-
     def dv_block(b, own=False):
         s = dot_nt(vall[me], uall[b])
         p = jnp.exp2(s * LOGIT_SCALE - wide(bcol[...])) * msgs[b, :, 0:ROWS]
@@ -401,6 +382,20 @@
             p = jnp.where(eye, p - 1.0, p)
         return dot_nn(p.astype(BF16), uall[b])
 
+    tower_backward(qx, wqo, a_q, h_q, u_q, r_q, gp_q)
+    pair_start(0, gp_q, pp_q)
+    gather_jobs(uall, 0, 2, s_u, m_u)
+    pair_send(uall, 1, s_u.at[1], m_ud)
+    dacc[...] = dv_block(me, True)
+    gather_jobs(uall, 1, 1, s_u, m_u)
+    pair_finish(0, gp_q, pp_q, ra_q)
+
+    arrived(msgs.at[0:NDEV - 1], m_msg.at[0])
+    total = msgs[0, :, ROWS:MSG]
+    for b in range(1, NDEV):
+        total = total + msgs[b, :, ROWS:MSG]
+    loss_out[...] = jnp.broadcast_to(jnp.sum(total, axis=1, keepdims=True) * (1.0 / TOTAL), (1, 128))
+
     def dv_group(blocks):
         total = dacc[...]
         for b in blocks:
@@ -410,7 +405,7 @@
     def dv_step(g, _):
         @pl.when(g == 1)
         def _():
-            gather_jobs(uall, u1[3:], s_u, m_u)
+            gather_jobs(uall, 1, 2, s_u, m_u)
             pair_send(uall, 2, s_u.at[1], m_ud)
             pair_wait(uall, 1, m_ud)
 
@@ -420,23 +415,22 @@
 
         @pl.when(g == 3)
         def _():
-            gather_jobs(uall, u2, s_u, m_u)
+            gather_jobs(uall, 2, 2, s_u, m_u)
             pair_send(uall, 3, s_u.at[1], m_ud)
             pair_wait(uall, 2, m_ud)
 
         @pl.when(g == 4)
         def _():
             pair_wait(uall, 3, m_ud)
-            r2_finish(0, gq_out, pp_q, rb_q)
 
         dv_group([nth_dev(3 * g + j) for j in range(3)])
         return 0
 
     pair_wait(uall, 0, m_ud)
-    dacc[...] = dv_block(me, True)
     lax.fori_loop(0, 5, dv_step, 0)
     tower_backward(vx, wvo, a_v, h_v, u_v, r_v, gp_v)
     pair_start(1, gp_v, pp_v)
+    r2_finish(0, gq_out, pp_q, rb_q)
     sent(vall.at[0:7], s_v.at[0])
     sent(lqall.at[0:7], s_v.at[1])
     sent(vall.at[0:8], s_v.at[2])
@@ -500,11 +494,11 @@
                 V((PACK, EMB), F32), V((PACK, EMB), F32),
                 V((HALF, EMB), F32), V((HALF, EMB), F32),
                 V((HALF // 2, EMB), F32), V((HALF // 2, EMB), F32),
-                V((3, HALF // 8, EMB), F32), V((3, HALF // 8, EMB), F32), V((2, HALF // 8, EMB), F32), dma((2, 3)),
+                V((3, HALF // 8, EMB), F32), V((3, HALF // 8, EMB), F32), V((2, HALF // 8, EMB), F32), dma((2,)),
                 dma((1,)), dma((1,)),
-                dma((4,)), dma((3, 8)), dma((4,)), dma((4,)), dma((2,)), dma((3, 8)), dma((4,)),
-                dma((2,)), dma((2,)), dma((2,)), dma((2, 3)), dma((2,)), dma((2, 3)),
-                dma((2,)), dma((2, 3, 3)), dma((2,)), dma((2, 3)), dma((2,)), dma((2,)),
+                dma((4,)), dma((6,)), dma((8,)), dma((4,)), dma((4,)), dma((2,)), dma((6,)), dma((4,)),
+                dma((2,)), dma((2,)), dma((2,)), dma((2,)), dma((2,)), dma((2,)),
+                dma((2,)), dma((2, 3)), dma((2,)), dma((2,)), dma((2,)), dma((2,)),
             ],
             compiler_params=pltpu.CompilerParams(collective_id=0, has_side_effects=True,
                                                  vmem_limit_bytes=48 * 1024 * 1024),

time: 49.1 us -> 47.9 us (0.976)
  Pallas kernels: 48.3 us -> 47.1 us
    pallas_call x1, Pallas kernels: 46.7 us -> 45.5 us  [local_step(): pl.pallas_call(kernel, out_shape=(shape((1, 128), F32), shape((PACK, EMB)...]
where the time goes in v5:
time: 47.9 us; the launch traced here: 47.8 us
  Pallas kernels  47.1 us (98%)
  between operations  0.64 us (1%)
    pallas_call x1, Pallas kernels, local_step(): pl.pallas_call(kernel, out_shape=(shape((1, 128), F32), shape((PACK, EMB)...  45.5 us
    pallas_call x1, Pallas kernels, local_step(): pl.pallas_call(finish, out_shape=(shape((1,), F32), shape((FEAT, HID), F3...  1.62 us

profile of v5, /device:TPU:0, one launch (start us, length us, event | category | flops | bytes accessed | tf_op | source)
XLA Modules:
  0.0 47.8 jit_solution(13248116379004924747)
XLA Ops:
  0.6 45.5 %step.1 = (f32[1,128]{1,0:T(1,128)S(1)}, f32[1280,128]{1,0:T(8,128)S(1)}, f32[1280,128]{1,0:T(8,128)S(1)}) custom-call(bf16[512,512]{1,0:T(8,128)(2,1)} %qx_h.1, bf16[512,512]{1,0:T(8,128)(2,1)} %vx_h.1, f32[1,512]{1,0:T(1,128)} %bitcast.1, bf16[512,256]{1,0:T(8,128)(2,1)} %wqi_h.1, bf16[256,128]{1,0:T(8,128)(2,1)} %wqo_h.1, bf16[512,256]{1,0:T(8,128)(2,1)} %wvi_h.1, ...), custom_call_target="tpu_custom_call" | custom-call | tf_op jit(solution)/shard_map/step/pallas_call | solution.py:477
  46.1 1.6 %finish.1 = (f32[1]{0:T(128)}, f32[512,256]{1,0:T(8,128)}, f32[256,128]{1,0:T(8,128)}, f32[512,256]{1,0:T(8,128)}, f32[256,128]{1,0:T(8,128)}) custom-call(f32[1,128]{1,0:T(1,128)S(1)} %get-tuple-element.8.loss, f32[1280,128]{1,0:T(8,128)S(1)} %get-tuple-element.9.gq, f32[1280,128]{1,0:T(8,128)S(1)} %get-tuple-element.10.gv), custom_call_target="tpu_custom_call" | custom-call | tf_op jit(solution)/shard_map/finish/pallas_call | solution.py:508

commit v6 on v5

--- a/solution.py
+++ b/solution.py
@@ -16,8 +16,8 @@
 EMB = 128
 PACK = 2 * FEAT + HID
 HALF = PACK // 2
-SUM_BASE = (0, 192, 384)
-SUM_ROWS = (192, 192, 256)
+SUM_BASE = (0, 448, 896)
+SUM_ROWS = (448, 448, 384)
 TOTAL = NDEV * ROWS
 GRAD_SCALE = 1.0 / (TEMPERATURE * TOTAL)
 LOGIT_SCALE = LOG2E / TEMPERATURE
@@ -44,15 +44,15 @@
 
 
 def wide(col):
-    return jnp.concatenate([col, col, col, col], axis=1)
+    return jnp.concatenate([col] * (ROWS // EMB), axis=1)
 
 
 def kernel(qx_h, vx_h, lq_h, wqi_h, wqo_h, wvi_h, wvo_h,
            loss_out, gq_out, gv_out,
            qx, vx, wqi, wqo, wvi, wvo, s_in,
-           uall, vall, lqall, crun, pos_row, msgs, lacc, diag,
-           a_q, a_v, h_q, h_v, u_q, u_v, r_q, r_v, invl, bcol, dacc,
-           gp_q, gp_v, pp_q, pp_v, ra_q, ra_v, rb_q, rb_v, fin, s_own,
+           uall, vall, lqall, crun, pos_row, msgs, lacc, diag, invl, bcol, dacc,
+           a_q, a_v, h_q, h_v, u_q, u_v, r_q, r_v,
+           gp_q, gp_v, pp, ra, rb, fin, s_own,
            s_msg, m_msg,
            s_v, m_v, m_l, m_vd, m_ld, s_u, m_u, m_ud,
            s_pair, m_pair, s_r1, m_r1, s_r2, m_r2, s_g1, m_g1, s_g2, m_g2, s_fw, m_fw):
@@ -149,8 +149,8 @@
                 arrived(lqall.at[dev(m)], ml.at[m])
                 for tt in range(t + 1, 3):
                     send_part(lqall, 3, m, tt, ss, ml)
-        for p, m in jobs:
-            for tt in range(t + 1, 3):
+        for tt in range(t + 1, 3):
+            for p, m in jobs:
                 send_part(ref, p, m, tt, ss, ms)
 
     def pair_send(ref, level, sd, md):
@@ -215,11 +215,12 @@
             pair_send(vall, 1, s_v.at[2], m_vd)
             pair_wait(lqall, 0, m_ld)
             pair_wait(vall, 0, m_vd)
+            gather_own(uall, (0,), s_u, m_u)
 
         @pl.when(g == 1)
         def _():
             gather_jobs(vall, 1, 1, s_v, m_v, m_l)
-            gather_own(uall, (0, 1, 2), s_u, m_u)
+            gather_own(uall, (1, 2), s_u, m_u)
             pair_wait(lqall, 1, m_ld)
             pair_wait(vall, 1, m_vd)
 
@@ -265,115 +266,101 @@
     dacc[...] = dacc[...] * invl[...] + (p_own - 1.0).astype(BF16).astype(F32) * vall[me].astype(F32)
     gather_jobs(uall, 0, 1, s_u, m_u)
 
-    def tower_backward(x, w_out, a_ref, h_ref, u_ref, r_ref, g):
-        du = dacc[...] * GRAD_SCALE
+    def tower_backward(owner, x, w_out, a_ref, h_ref, u_ref, r_ref, g):
+        d_unit = dacc[...] * GRAD_SCALE
         u = u_ref[...]
-        de = (r_ref[...] * (du - u * jnp.sum(u * du, axis=-1, keepdims=True))).astype(BF16)
+        de = (r_ref[...] * (d_unit - u * jnp.sum(u * d_unit, axis=-1, keepdims=True))).astype(BF16)
         g[2 * FEAT:PACK, :] = dot_tn(h_ref[...], de)
+        hand_over(owner, g, GO)
         dh = dot_nt(de, w_out[...])
         da = jnp.where(a_ref[...] > 0, dh, 0.0).astype(BF16)
         gi = dot_tn(x[...], da)
         g[0:FEAT, :] = gi[:, 0:EMB]
         g[FEAT:2 * FEAT, :] = gi[:, EMB:HID]
+        hand_over(owner, g, GI)
 
     bit = {1: bit_x, 2: bit_y, 4: bit_z}
     PLANE = ((0, 1), (1, 0), (1, 1))
 
-    def rows(base, size):
-        return pl.ds(pl.multiple_of(base, 8), size)
-
     def slot(p, b0, b1, b2, count):
         eighth = SUM_ROWS[p] // 8
-        return rows(SUM_BASE[p] + (b0 * 4 + b1 * 2 + b2) * eighth, count * eighth)
-
-    def half(c):
-        return rows(c * HALF, HALF)
-
-    def out_slot(c, p, b0, b1, b2, count):
-        eighth = SUM_ROWS[p] // 8
-        return rows(c * HALF + SUM_BASE[p] + (b0 * 4 + b1 * 2 + b2) * eighth, count * eighth)
-
-    def bits(p, f1=0, f2=0):
-        d0, d1, d2 = ORDERS[p]
-        b1 = bit[d1] if not f1 else 1 - bit[d1]
-        b2 = bit[d2] if not f2 else 1 - bit[d2]
-        return bit[d0], b1, b2
+        return pl.ds(pl.multiple_of(SUM_BASE[p] + (b0 * 4 + b1 * 2 + b2) * eighth, 8), count * eighth)
+
+    def part(p, share):
+        return pl.ds(SUM_BASE[p] // share, SUM_ROWS[p] // share)
+
+    def bits(p, flip=(0, 0)):
+        b = [bit[d] for d in ORDERS[p]]
+        return (b[0],) + tuple(1 - v if f else v for v, f in zip(b[1:], flip))
 
     def plane_dev(p, k):
         return dev(PLANE[k][0] * ORDERS[p][1] + PLANE[k][1] * ORDERS[p][2])
 
     def plane_shard(out, p, k):
-        return out.at[out_slot(core, p, *bits(p, *PLANE[k]), 1), :]
+        return out.at[slot(p, *bits(p, PLANE[k]), 1), :]
 
     def axis_half(out, p, far):
         b0 = bits(p)[0]
-        return out.at[out_slot(core, p, 1 - b0 if far else b0, 0, 0, 4), :]
-
-    def pair_start(t, g, pp):
-        send(g.at[half(1 - core), :], pp, s_pair.at[t], m_pair.at[t], partner)
-
-    def pair_finish(t, g, pp, ra):
-        arrived(pp, m_pair.at[t])
-        pp[...] = pp[...] + g[half(core), :]
-        for p in range(3):
-            part = ra.at[pl.ds(SUM_BASE[p] // 2, SUM_ROWS[p] // 2), :]
-            send(pp.at[slot(p, 1 - bits(p)[0], 0, 0, 4), :], part, s_r1.at[t], m_r1.at[t], dev(ORDERS[p][0]))
-
-    def r1_finish(t, pp, ra, rb):
-        arrived(ra, m_r1.at[t])
-        for p in range(3):
-            part = pl.ds(SUM_BASE[p] // 2, SUM_ROWS[p] // 2)
-            b0, _, _ = bits(p)
-            mine = slot(p, b0, 0, 0, 4)
-            pp[mine, :] = pp[mine, :] + ra[part, :]
+        return out.at[slot(p, 1 - b0 if far else b0, 0, 0, 4), :]
+
+    GO, GI = pl.ds(2 * FEAT, HID), pl.ds(0, 2 * FEAT)
+
+    def hand_over(owner, g, rows):
+        @pl.when(core != owner)
+        def _():
+            send(g.at[rows, :], pp.at[rows, :], s_pair, m_pair, partner)
+
+    def sum_pair(g):
+        arrived(pp, m_pair)
+        pp[...] = pp[...] + g[...]
+        for p in range(3):
+            send(pp.at[slot(p, 1 - bits(p)[0], 0, 0, 4), :], ra.at[part(p, 2), :], s_r1, m_r1, dev(ORDERS[p][0]))
+
+    def sum_axis():
+        arrived(ra, m_r1)
+        for p in range(3):
+            mine = slot(p, bits(p)[0], 0, 0, 4)
+            pp[mine, :] = pp[mine, :] + ra[part(p, 2), :]
         for k in (2, 0, 1):
             for p in range(3):
-                part = rb.at[k, pl.ds(SUM_BASE[p] // 8, SUM_ROWS[p] // 8), :]
-                send(pp.at[slot(p, *bits(p, *PLANE[k]), 1), :], part, s_r2.at[t], m_r2.at[t], plane_dev(p, k))
-
-    def r2_finish(t, out, pp, rb):
-        arrived(rb, m_r2.at[t])
-        for p in range(3):
-            part = pl.ds(SUM_BASE[p] // 8, SUM_ROWS[p] // 8)
+                send(pp.at[slot(p, *bits(p, PLANE[k]), 1), :], rb.at[k, part(p, 8), :], s_r2, m_r2, plane_dev(p, k))
+
+    def sum_plane(out):
+        arrived(rb, m_r2)
+        for p in range(3):
             total = pp[slot(p, *bits(p), 1), :]
             for k in range(3):
-                total = total + rb[k, part, :]
-            own = fin.at[t, pl.ds(SUM_BASE[p] // 8, SUM_ROWS[p] // 8), :]
-            fin[t, SUM_BASE[p] // 8:(SUM_BASE[p] + SUM_ROWS[p]) // 8, :] = total
-            place = out.at[out_slot(core, p, *bits(p), 1), :]
-            keep = pltpu.make_async_copy(own, place, s_own.at[t])
-            keep.start()
-            for k in (2, 0, 1):
-                send(own, place, s_g1.at[t], m_g1.at[t, k], plane_dev(p, k))
-            send(own, place, s_g2.at[t], m_g2.at[t], dev(ORDERS[p][0]))
-
-    def ag_plane(t, out):
+                total = total + rb[k, part(p, 8), :]
+            fin[part(p, 8), :] = total
+        for k in (2, 0, 1):
+            for p in range(3):
+                send(fin.at[part(p, 8), :], out.at[slot(p, *bits(p), 1), :], s_g1, m_g1.at[k], plane_dev(p, k))
+        for p in range(3):
+            place = out.at[slot(p, *bits(p), 1), :]
+            send(fin.at[part(p, 8), :], place, s_g2, m_g2, dev(ORDERS[p][0]))
+            pltpu.make_async_copy(fin.at[part(p, 8), :], place, s_own).start()
+
+    def spread_plane(out):
         for k in range(3):
-            arrived(out.at[0:HALF // 8, :], m_g1.at[t, k])
+            arrived(fin, m_g1.at[k])
             for p in range(3):
                 ref = plane_shard(out, p, k)
-                send(ref, ref, s_g2.at[t], m_g2.at[t], dev(ORDERS[p][0]))
-        pltpu.make_async_copy(fin.at[t], out.at[0:HALF // 8, :], s_own.at[t]).wait()
+                send(ref, ref, s_g2, m_g2, dev(ORDERS[p][0]))
+        pltpu.make_async_copy(fin, out.at[part(0, 1), :].at[0:HALF // 4, :], s_own).wait()
         for p in range(3):
             ref = axis_half(out, p, 0)
-            send(ref, ref, s_fw.at[t], m_fw.at[t], partner)
-
-    def ag_axis(t, out):
-        arrived(out.at[0:HALF // 2, :], m_g2.at[t])
+            send(ref, ref, s_fw, m_fw, partner)
+
+    def spread_axis(out):
+        arrived(ra, m_g2)
         for p in range(3):
             ref = axis_half(out, p, 1)
-            send(ref, ref, s_fw.at[t], m_fw.at[t], partner)
-
-    def ag_finish(t, out):
-        arrived(out.at[0:HALF, :], m_fw.at[t])
-
-    def sums_sent(t, out, pp, ra, rb):
-        sent(pp, s_pair.at[t])
-        sent(ra, s_r1.at[t])
-        sent(rb, s_r2.at[t])
-        sent(rb, s_g1.at[t])
-        sent(ra, s_g2.at[t])
-        sent(pp, s_fw.at[t])
+            send(ref, ref, s_fw, m_fw, partner)
+
+    def on_core(owner, stage, *args):
+        @pl.when(core == owner)
+        def _():
+            stage(*args)
 
     def dv_block(b, own=False):
         s = dot_nt(vall[me], uall[b])
@@ -382,13 +369,12 @@
             p = jnp.where(eye, p - 1.0, p)
         return dot_nn(p.astype(BF16), uall[b])
 
-    tower_backward(qx, wqo, a_q, h_q, u_q, r_q, gp_q)
-    pair_start(0, gp_q, pp_q)
+    tower_backward(0, qx, wqo, a_q, h_q, u_q, r_q, gp_q)
     gather_jobs(uall, 0, 2, s_u, m_u)
     pair_send(uall, 1, s_u.at[1], m_ud)
     dacc[...] = dv_block(me, True)
     gather_jobs(uall, 1, 1, s_u, m_u)
-    pair_finish(0, gp_q, pp_q, ra_q)
+    on_core(0, sum_pair, gp_q)
 
     arrived(msgs.at[0:NDEV - 1], m_msg.at[0])
     total = msgs[0, :, ROWS:MSG]
@@ -411,7 +397,7 @@
 
         @pl.when(g == 2)
         def _():
-            r1_finish(0, pp_q, ra_q, rb_q)
+            on_core(0, sum_axis)
 
         @pl.when(g == 3)
         def _():
@@ -428,9 +414,8 @@
 
     pair_wait(uall, 0, m_ud)
     lax.fori_loop(0, 5, dv_step, 0)
-    tower_backward(vx, wvo, a_v, h_v, u_v, r_v, gp_v)
-    pair_start(1, gp_v, pp_v)
-    r2_finish(0, gq_out, pp_q, rb_q)
+    tower_backward(1, vx, wvo, a_v, h_v, u_v, r_v, gp_v)
+    on_core(0, sum_plane, gq_out)
     sent(vall.at[0:7], s_v.at[0])
     sent(lqall.at[0:7], s_v.at[1])
     sent(vall.at[0:8], s_v.at[2])
@@ -438,17 +423,17 @@
     sent(uall.at[0:7], s_u.at[0])
     sent(uall.at[0:8], s_u.at[1])
     sent(msgs.at[0:NDEV - 1], s_msg.at[0])
-    pair_finish(1, gp_v, pp_v, ra_v)
-    ag_plane(0, gq_out)
-    r1_finish(1, pp_v, ra_v, rb_v)
-    ag_axis(0, gq_out)
-    r2_finish(1, gv_out, pp_v, rb_v)
-    ag_finish(0, gq_out)
-    sums_sent(0, gq_out, pp_q, ra_q, rb_q)
-    ag_plane(1, gv_out)
-    ag_axis(1, gv_out)
-    ag_finish(1, gv_out)
-    sums_sent(1, gv_out, pp_v, ra_v, rb_v)
+    on_core(1, sum_pair, gp_v)
+    on_core(0, spread_plane, gq_out)
+    on_core(1, sum_axis)
+    on_core(0, spread_axis, gq_out)
+    on_core(1, sum_plane, gv_out)
+    on_core(1, spread_plane, gv_out)
+    on_core(1, spread_axis, gv_out)
+    sent(pp, s_pair)
+    for like, ssem in ((ra, s_r1), (rb, s_r2), (rb, s_g1), (ra, s_g2), (pp, s_fw)):
+        sent(like, ssem)
+    arrived(pp, m_fw)
 
 
 def finish(loss, gq, gv, loss_out, gqi, gqo, gvi, gvo, sem):
@@ -479,27 +464,16 @@
             out_shape=(shape((1, 128), F32), shape((PACK, EMB), F32), shape((PACK, EMB), F32)),
             in_specs=[hbm] * 7,
             out_specs=(vmem, anym, anym),
-            scratch_shapes=[
-                V((ROWS, FEAT), BF16), V((ROWS, FEAT), BF16),
-                V((FEAT, HID), BF16), V((HID, EMB), BF16), V((FEAT, HID), BF16), V((HID, EMB), BF16), dma((7,)),
-                V((NDEV, ROWS, EMB), BF16), V((NDEV, ROWS, EMB), BF16),
-                V((NDEV, 1, ROWS), F32), V((1, 128), F32), V((1, ROWS), F32),
-                V((NDEV, 1, MSG), F32),
-                V((ROWS, EMB), F32), V((ROWS, EMB), F32),
-                V((ROWS, HID), F32), V((ROWS, HID), F32),
-                V((ROWS, HID), BF16), V((ROWS, HID), BF16),
-                V((ROWS, EMB), F32), V((ROWS, EMB), F32),
-                V((ROWS, EMB), F32), V((ROWS, EMB), F32),
-                V((ROWS, EMB), F32), V((ROWS, EMB), F32), V((ROWS, EMB), F32),
-                V((PACK, EMB), F32), V((PACK, EMB), F32),
-                V((HALF, EMB), F32), V((HALF, EMB), F32),
-                V((HALF // 2, EMB), F32), V((HALF // 2, EMB), F32),
-                V((3, HALF // 8, EMB), F32), V((3, HALF // 8, EMB), F32), V((2, HALF // 8, EMB), F32), dma((2,)),
-                dma((1,)), dma((1,)),
-                dma((4,)), dma((6,)), dma((8,)), dma((4,)), dma((4,)), dma((2,)), dma((6,)), dma((4,)),
-                dma((2,)), dma((2,)), dma((2,)), dma((2,)), dma((2,)), dma((2,)),
-                dma((2,)), dma((2, 3)), dma((2,)), dma((2,)), dma((2,)), dma((2,)),
-            ],
+            scratch_shapes=(
+                [V((ROWS, FEAT), BF16)] * 2 + [V((FEAT, HID), BF16), V((HID, EMB), BF16)] * 2 + [dma((7,))]
+                + [V((NDEV, ROWS, EMB), BF16)] * 2
+                + [V((NDEV, 1, ROWS), F32), V((1, EMB), F32), V((1, ROWS), F32), V((NDEV, 1, MSG), F32)]
+                + [V((ROWS, EMB), F32)] * 5
+                + [V((ROWS, HID), F32)] * 2 + [V((ROWS, HID), BF16)] * 2 + [V((ROWS, EMB), F32)] * 4
+                + [V((PACK, EMB), F32)] * 3 + [V((HALF, EMB), F32), V((3, HALF // 4, EMB), F32), V((HALF // 4, EMB), F32)]
+                + [dma]
+                + [dma((1,))] * 2 + [dma((n,)) for n in (4, 6, 8, 4, 4, 2, 6, 4)]
+                + [dma] * 7 + [dma((3,))] + [dma] * 4),
             compiler_params=pltpu.CompilerParams(collective_id=0, has_side_effects=True,
                                                  vmem_limit_bytes=48 * 1024 * 1024),
             name="step",

time: 47.9 us -> 45.9 us (0.958)
  Pallas kernels: 47.1 us -> 45.1 us
    pallas_call x1, Pallas kernels: 45.5 us -> 43.5 us  [local_step(): pl.pallas_call(kernel, out_shape=(shape((1, 128), F32), shape((PACK, EMB)...]
where the time goes in v6:
time: 45.9 us; the launch traced here: 45.8 us
  Pallas kernels  45.1 us (98%)
  between operations  0.64 us (1%)
    pallas_call x1, Pallas kernels, local_step(): pl.pallas_call(kernel, out_shape=(shape((1, 128), F32), shape((PACK, EMB)...  43.5 us
    pallas_call x1, Pallas kernels, local_step(): pl.pallas_call(finish, out_shape=(shape((1,), F32), shape((FEAT, HID), F3...  1.62 us

profile of v6, /device:TPU:0, one launch (start us, length us, event | category | flops | bytes accessed | tf_op | source)
XLA Modules:
  0.0 45.8 jit_solution(2307025864958883739)
XLA Ops:
  0.6 43.5 %step.1 = (f32[1,128]{1,0:T(1,128)S(1)}, f32[1280,128]{1,0:T(8,128)S(1)}, f32[1280,128]{1,0:T(8,128)S(1)}) custom-call(bf16[512,512]{1,0:T(8,128)(2,1)} %qx_h.1, bf16[512,512]{1,0:T(8,128)(2,1)} %vx_h.1, f32[1,512]{1,0:T(1,128)} %bitcast.1, bf16[512,256]{1,0:T(8,128)(2,1)} %wqi_h.1, bf16[256,128]{1,0:T(8,128)(2,1)} %wqo_h.1, bf16[512,256]{1,0:T(8,128)(2,1)} %wvi_h.1, ...), custom_call_target="tpu_custom_call" | custom-call | tf_op jit(solution)/shard_map/step/pallas_call | solution.py:462
  44.1 1.6 %finish.1 = (f32[1]{0:T(128)}, f32[512,256]{1,0:T(8,128)}, f32[256,128]{1,0:T(8,128)}, f32[512,256]{1,0:T(8,128)}, f32[256,128]{1,0:T(8,128)}) custom-call(f32[1,128]{1,0:T(1,128)S(1)} %get-tuple-element.8.loss, f32[1280,128]{1,0:T(8,128)S(1)} %get-tuple-element.9.gq, f32[1280,128]{1,0:T(8,128)S(1)} %get-tuple-element.10.gv), custom_call_target="tpu_custom_call" | custom-call | tf_op jit(solution)/shard_map/finish/pallas_call | solution.py:482

commit v7 on v6

--- a/solution.py
+++ b/solution.py
@@ -436,22 +436,21 @@
     arrived(pp, m_fw)
 
 
-def finish(loss, gq, gv, loss_out, gqi, gqo, gvi, gvo, sem):
-    copies = []
-    for i, (g, gi, go) in enumerate(((gq, gqi, gqo), (gv, gvi, gvo))):
-        copies.append(pltpu.make_async_copy(g.at[0:FEAT, :], gi.at[:, 0:EMB], sem.at[i, 0]))
-        copies.append(pltpu.make_async_copy(g.at[FEAT:2 * FEAT, :], gi.at[:, EMB:HID], sem.at[i, 1]))
-        copies.append(pltpu.make_async_copy(g.at[2 * FEAT:PACK, :], go, sem.at[i, 2]))
+def finish(loss, gq, gv, loss_out, gqi, gqo, gvi, gvo, scalar, sem):
+    scalar[0] = loss[0, 0]
+    copies = [(scalar, loss_out)]
+    for g, gi, go in ((gq, gqi, gqo), (gv, gvi, gvo)):
+        copies += [(g.at[0:FEAT, :], gi.at[:, 0:EMB]), (g.at[FEAT:2 * FEAT, :], gi.at[:, EMB:HID]),
+                   (g.at[2 * FEAT:PACK, :], go)]
+    copies = [pltpu.make_async_copy(src, dst, sem.at[n]) for n, (src, dst) in enumerate(copies)]
     for copy in copies:
         copy.start()
-    loss_out[0] = loss[0, 0]
     for copy in copies:
         copy.wait()
 
 
 def solution(mesh):
     vmem = pl.BlockSpec(memory_space=pltpu.VMEM)
-    smem = pl.BlockSpec(memory_space=pltpu.SMEM)
     hbm = pl.BlockSpec(memory_space=pltpu.HBM)
     anym = pl.BlockSpec(memory_space=pl.ANY)
     dma = pltpu.SemaphoreType.DMA
@@ -484,8 +483,8 @@
             out_shape=(shape((1,), F32), shape((FEAT, HID), F32), shape((HID, EMB), F32),
                        shape((FEAT, HID), F32), shape((HID, EMB), F32)),
             in_specs=[vmem, anym, anym],
-            out_specs=(smem, hbm, hbm, hbm, hbm),
-            scratch_shapes=[dma((2, 3))],
+            out_specs=(hbm,) * 5,
+            scratch_shapes=[pltpu.SMEM((1,), F32), dma((7,))],
             compiler_params=pltpu.CompilerParams(vmem_limit_bytes=8 * 1024 * 1024),
             name="finish",
         )(loss, gq, gv)

time: 45.9 us -> 45.4 us (0.989)
  Pallas kernels: 45.1 us -> 44.6 us
    pallas_call x1, Pallas kernels: 1.62 us -> 1.14 us  [local_step(): pl.pallas_call(finish, out_shape=(shape((1,), F32), shape((FEAT, HID), F3...]
where the time goes in v7:
time: 45.4 us; the launch traced here: 45.3 us
  Pallas kernels  44.6 us (98%)
  between operations  0.64 us (1%)
    pallas_call x1, Pallas kernels, local_step(): pl.pallas_call(kernel, out_shape=(shape((1, 128), F32), shape((PACK, EMB)...  43.5 us
    pallas_call x1, Pallas kernels, local_step(): pl.pallas_call(finish, out_shape=(shape((1,), F32), shape((FEAT, HID), F3...  1.14 us

profile of v7, /device:TPU:0, one launch (start us, length us, event | category | flops | bytes accessed | tf_op | source)
XLA Modules:
  0.0 45.3 jit_solution(9914777467013616743)
XLA Ops:
  0.6 43.5 %step.1 = (f32[1,128]{1,0:T(1,128)S(1)}, f32[1280,128]{1,0:T(8,128)S(1)}, f32[1280,128]{1,0:T(8,128)S(1)}) custom-call(bf16[512,512]{1,0:T(8,128)(2,1)} %qx_h.1, bf16[512,512]{1,0:T(8,128)(2,1)} %vx_h.1, f32[1,512]{1,0:T(1,128)} %bitcast.1, bf16[512,256]{1,0:T(8,128)(2,1)} %wqi_h.1, bf16[256,128]{1,0:T(8,128)(2,1)} %wqo_h.1, bf16[512,256]{1,0:T(8,128)(2,1)} %wvi_h.1, ...), custom_call_target="tpu_custom_call" | custom-call | tf_op jit(solution)/shard_map/step/pallas_call | solution.py:461
  44.1 1.1 %finish.1 = (f32[1]{0:T(128)}, f32[512,256]{1,0:T(8,128)}, f32[256,128]{1,0:T(8,128)}, f32[512,256]{1,0:T(8,128)}, f32[256,128]{1,0:T(8,128)}) custom-call(f32[1,128]{1,0:T(1,128)S(1)} %get-tuple-element.8.loss, f32[1280,128]{1,0:T(8,128)S(1)} %get-tuple-element.9.gq, f32[1280,128]{1,0:T(8,128)S(1)} %get-tuple-element.10.gv), custom_call_target="tpu_custom_call" | custom-call | tf_op jit(solution)/shard_map/finish/pallas_call | solution.py:481
